TPU v7x, 128 devices: a whole 4x4x4 slice. The times are simulated.
128 devices in a mesh: dp: 1, tp: 2 (over core), sp: 64 (over z, y, x).
Axes of the slice: x: 4, y: 4, z: 4, core: 2. Of those that a mesh axis runs over, the one named last changes fastest.
Arguments:
- hidden: bfloat16 [65536, 1024], P(('dp', 'sp'))
- w_query: bfloat16 [1024, 1024], P(None, 'tp')
- w_key: bfloat16 [1024, 1024], P(None, 'tp')
- w_value: bfloat16 [1024, 1024], P(None, 'tp')
- w_out: bfloat16 [1024, 1024], P('tp')
- branch_bias: float32 [4, 16], replicated
Outputs:
- output: bfloat16 [65536, 1024], P(('dp', 'sp'), 'tp')
All inputs are finite; a program needn't handle non-finite values.
Results may differ from a plain program's by a relative error of at most 0.00241.
Values are sent between devices in bfloat16 or wider.
A program may use at most 1 GiB of HBM per device.

v0:
```python
import jax
import jax.numpy as jnp
from jax import lax
from jax.sharding import PartitionSpec as P

SEG_BASE = 2048


def attend(q_sel, k_sel, v_sel, logit_scale):
    logits = jnp.einsum('hasd,hatd->hast', q_sel, k_sel, preferred_element_type=jnp.float32) * logit_scale
    row_max = jnp.max(logits, axis=-1, keepdims=True)
    weights = jnp.exp(logits - row_max)
    row_sum = jnp.sum(weights, axis=-1, keepdims=True)
    numer_sum = jnp.einsum('hast,hatd->hasd', weights.astype(jnp.bfloat16), v_sel, preferred_element_type=jnp.float32)
    return numer_sum / row_sum, (row_max + jnp.log(row_sum))[..., 0]


def solution(mesh):
    seq_size = mesh.shape['sp']
    head_groups = mesh.shape['tp']

    def device_fn(hidden, w_query, w_key, w_value, w_out, branch_bias):
        tokens, model_width = hidden.shape
        num_branches, num_heads = branch_bias.shape
        head_dim = model_width // num_heads
        local_heads = num_heads // head_groups
        logit_scale = head_dim ** -0.5
        head_start = lax.axis_index('tp') * local_heads
        head_ids = head_start + jnp.arange(local_heads)
        bias_local = lax.dynamic_slice_in_dim(branch_bias, head_start, local_heads, axis=1)

        def project(weight):
            return jnp.dot(hidden, weight, preferred_element_type=jnp.float32).astype(jnp.bfloat16).reshape(tokens, local_heads, head_dim)

        q_loc = project(w_query)
        k_loc = project(w_key)
        v_loc = project(w_value)
        for branch in range(num_branches):
            value_a8 = 2 ** branch
            seg_len = SEG_BASE * value_a8
            kept_rows = tokens // value_a8
            phase_ok = head_ids[:, None] % value_a8 == jnp.arange(value_a8)[None, :]
            phase_bf = phase_ok.astype(jnp.bfloat16)
            phase_f = phase_ok.astype(jnp.float32)

            def pick_rows(source):
                split_rows = source.reshape(kept_rows, value_a8, local_heads, head_dim)
                return jnp.einsum('sihd,hi->hsd', split_rows, phase_bf, preferred_element_type=jnp.float32).astype(jnp.bfloat16)

            q_sel = pick_rows(q_loc)
            k_sel = pick_rows(k_loc)
            v_sel = pick_rows(v_loc)
            if seg_len <= tokens:
                seg_shape = (local_heads, tokens // seg_len, SEG_BASE, head_dim)
                attn_out, log_norm = attend(q_sel.reshape(seg_shape), k_sel.reshape(seg_shape), v_sel.reshape(seg_shape), logit_scale)
            else:
                group_len = seg_len // tokens
                k_parts = [k_sel]
                v_parts = [v_sel]
                for shift_by in range(1, group_len):
                    pairs_list = [(source_dev, (source_dev // group_len) * group_len + (source_dev + shift_by) % group_len) for source_dev in range(seq_size)]
                    k_parts.append(lax.ppermute(k_sel, 'sp', pairs_list))
                    v_parts.append(lax.ppermute(v_sel, 'sp', pairs_list))
                k_seg = jnp.concatenate(k_parts, axis=1)[:, None]
                v_seg = jnp.concatenate(v_parts, axis=1)[:, None]
                attn_out, log_norm = attend(q_sel[:, None], k_seg, v_seg, logit_scale)
            out_full = jnp.einsum('hsd,hi->sihd', attn_out.reshape(local_heads, kept_rows, head_dim), phase_f).reshape(tokens, local_heads, head_dim)
            lse_full = jnp.einsum('hs,hi->sih', log_norm.reshape(local_heads, kept_rows), phase_f).reshape(tokens, local_heads)
            mask_full = jnp.broadcast_to(phase_ok.T[None], (kept_rows, value_a8, local_heads)).reshape(tokens, local_heads)
            branch_score = jnp.where(mask_full, lse_full + bias_local[branch][None, :], -jnp.inf)
            if branch == 0:
                run_num = out_full
                run_max = branch_score
                run_den = jnp.ones_like(branch_score)
            else:
                new_max = jnp.maximum(run_max, branch_score)
                keep_old = jnp.exp(run_max - new_max)
                take_new = jnp.exp(branch_score - new_max)
                run_num = run_num * keep_old[..., None] + out_full * take_new[..., None]
                run_den = run_den * keep_old + take_new
                run_max = new_max
        combined = (run_num / run_den[..., None]).astype(jnp.bfloat16).reshape(tokens, local_heads * head_dim)
        part_out = jnp.dot(combined, w_out, preferred_element_type=jnp.float32)
        reduced = lax.psum_scatter(part_out, 'tp', scatter_dimension=1, tiled=True)
        return reduced.astype(jnp.bfloat16)

    return jax.shard_map(device_fn, mesh=mesh, in_specs=(P(('dp', 'sp'), None), P(None, 'tp'), P(None, 'tp'), P(None, 'tp'), P('tp', None), P(None, None)), out_specs=P(('dp', 'sp'), 'tp'), check_vma=False)
```

profile of v0, /device:TPU:1, one launch (start us, length us, event | category | flops | bytes accessed | tf_op | source)
XLA Modules:
  0.0 490.2 jit_solution(13951902867826536961)
XLA Ops:
  31.9 6.4 %multiply_reduce_fusion.6 = (bf16[8,128,64]{2,0,1:T(8,128)(2,1)}, bf16[8,128,64]{2,0,1:T(8,128)(2,1)S(1)}, bf16[8,128,64]{2,0,1:T(8,128)(2,1)}) fusion(f32[8,8]{0,1:T(8,128)S(1)} %get-tuple-element.26, bf16[128,8,8,64]{3,2,1,0:T(8,128)(2,1)} %reshape_reshape.36, bf16[128,8,8,64]{3,2,1,0:T(8,128)(2,1)} %reshape_reshape.37, ...), kind=kLoop, calls=%fused_computation.22 | loop fusion | flops 4521984 | bytes 3539200
  62.9 6.1 %multiply_reduce_fusion.9 = (bf16[8,256,64]{2,0,1:T(8,128)(2,1)}, bf16[8,256,64]{2,0,1:T(8,128)(2,1)S(1)}, bf16[8,256,64]{2,0,1:T(8,128)(2,1)S(1)}) fusion(f32[8,4]{0,1:T(4,128)S(1)} %fusion.73, bf16[256,4,8,64]{3,2,1,0:T(8,128)(2,1)} %reshape_reshape.33, bf16[256,4,8,64]{3,2,1,0:T(8,128)(2,1)} %reshape_reshape.34, bf16[256,4,8,64]{3,2,1,0:T(8,128)(2,1)} %reshape_reshape.35), kind=kLoop, calls=%fused_computation.25 | loop fusion | flops 4325376 | bytes 3932288
  71.9 6.4 %multiply_reduce_fusion.12 = (bf16[8,512,64]{2,0,1:T(8,128)(2,1)}, bf16[8,512,64]{2,0,1:T(8,128)(2,1)S(1)}, bf16[8,512,64]{2,0,1:T(8,128)(2,1)}) fusion(f32[8,2]{0,1:T(2,128)S(1)} %compare_convert_fusion, bf16[512,2,8,64]{3,2,1,0:T(8,128)(2,1)S(1)} %copy-done.4, bf16[512,2,8,64]{3,2,1,0:T(8,128)(2,1)} %reshape_reshape.31, ...), kind=kLoop, calls=%fused_computation.28 | loop fusion | flops 3932160 | bytes 4718656
  108.7 4.6 collective-permute-done.27
  113.3 8.6 %collective-permute-start.29 = (bf16[8,128,64]{1,2,0:T(8,128)(2,1)}, bf16[8,128,64]{1,2,0:T(8,128)(2,1)S(1)}, u32[]{:S(2)}, u32[]{:S(2)}) collective-permute-start(bf16[8,128,64]{1,2,0:T(8,128)(2,1)} %copy.125), channel_id=1, source_target_pairs={{0,8},{1,9},{2,10},{3,11},{4,12},{5,13},{6,14},{7,15},{8,0},{9,1},... | collective-permute-start | bytes 393224 | tf_op jit(solution)/shard_map/ppermute | solution.py:62
  140.4 5.5 %collective-permute-start.35 = (bf16[8,128,64]{1,2,0:T(8,128)(2,1)}, bf16[8,128,64]{1,2,0:T(8,128)(2,1)S(1)}, u32[]{:S(2)}, u32[]{:S(2)}) collective-permute-start(bf16[8,128,64]{1,2,0:T(8,128)(2,1)} %copy.125), channel_id=1, source_target_pairs={{0,14},{1,15},{2,0},{3,1},{4,2},{5,3},{6,4},{7,5},{8,6},{9,7},{10,... | collective-permute-start | bytes 393224 | tf_op jit(solution)/shard_map/ppermute | solution.py:62
  159.5 5.1 %collective-permute-start.44 = (bf16[8,128,64]{1,2,0:T(8,128)(2,1)}, bf16[8,128,64]{1,2,0:T(8,128)(2,1)S(1)}, u32[]{:S(2)}, u32[]{:S(2)}) collective-permute-start(bf16[8,128,64]{1,2,0:T(8,128)(2,1)} %copy.131), channel_id=1, source_target_pairs={{0,8},{1,9},{2,10},{3,11},{4,12},{5,13},{6,14},{7,15},{8,0},{9,1},... | collective-permute-start | bytes 393224 | tf_op jit(solution)/shard_map/ppermute | solution.py:63
  177.8 4.7 collective-permute-start.16
  182.9 5.5 %collective-permute-start.10 = (bf16[8,256,64]{1,2,0:T(8,128)(2,1)S(1)}, bf16[8,256,64]{1,2,0:T(8,128)(2,1)}, u32[]{:S(2)}, u32[]{:S(2)}) collective-permute-start(bf16[8,256,64]{1,2,0:T(8,128)(2,1)S(1)} %copy-done.12), channel_id=1, source_target_pairs={{0,3},{1,4},{2,5},{3,6},{4,7},{5,0},{6,1},{7,2},{8,11},{9,12},{10,... | collective-permute-start | bytes 786440 | tf_op jit(solution)/shard_map/ppermute | solution.py:62
  193.2 4.8 reshape.835
  213.7 4.5 collective-permute-done.13
  225.5 4.1 multiply_reduce_fusion.2
  251.3 10.2 %fusion.55 = f32[8,256,64]{1,2,0:T(8,128)} fusion(bf16[8,2048,64]{1,2,0:T(8,128)(2,1)} %constant_dynamic-update-slice_fusion.8, f32[8,256,2048]{2,1,0:T(8,128)} %copy-done.2, f32[8,256]{1,0:T(8,128)S(1)} %get-tuple-element.29, f32[8,256]{1,0:T(8,128)S(1)} %fusion.9), kind=kOutput, calls=%fused_computation.72 | convolution fusion | flops 549584896 | bytes 19415040 | tf_op jit(solution)/shard_map/hast,hatd->hasd/dot_general | solution.py:14
  265.6 4.8 reshape.832
  274.8 8.9 %collective-permute-start.1 = (bf16[8,1024,64]{1,2,0:T(8,128)(2,1)}, bf16[8,1024,64]{1,2,0:T(8,128)(2,1)}, u32[]{:S(2)}, u32[]{:S(2)}) collective-permute-start(bf16[8,1024,64]{1,2,0:T(8,128)(2,1)} %bitcast.144), channel_id=1, source_target_pairs={{0,1},{1,0},{2,3},{3,2},{4,5},{5,4},{6,7},{7,6},{8,9},{9,8},{10,11... | collective-permute-start | bytes 3145736 | tf_op jit(solution)/shard_map/ppermute | solution.py:63
  283.7 14.7 %multiply_reduce_fusion.1 = (f32[8,512]{1,0:T(8,128)S(1)}, f32[8,512,2048]{2,1,0:T(8,128)}) fusion(bf16[8,512,64]{1,2,0:T(8,128)(2,1)S(1)} %copy-done.7, bf16[8,512,64]{1,2,0:T(8,128)(2,1)} %collective-permute-done.4, bf16[8,512,64]{1,2,0:T(8,128)(2,1)} %collective-permute-done.3, bf16[8,512,64]{1,2,0:T(8,128)(2,1)} %collective-permute-done.2, ...), kind=kOutput, calls=%fused_computation.6 | convolution fusion | flops 1098903552 | bytes 36192256 | tf_op jit(solution)/shard_map/hasd,hatd->hast/dot_general | solution.py:10
  298.4 14.0 %fusion.5 = f32[8,512]{1,0:T(8,128)S(1)} fusion(f32[8,512,2048]{2,1,0:T(8,128)} %get-tuple-element.32, f32[8,512]{1,0:T(8,128)S(1)} %get-tuple-element.31), kind=kLoop, calls=%fused_computation.8 | loop fusion | flops 25161728 | bytes 33587200 | tf_op jit(solution)/shard_map/reduce_sum | solution.py:13
  312.5 14.2 %fusion.58 = f32[8,512,64]{1,2,0:T(8,128)S(1)} fusion(bf16[8,512,64]{1,2,0:T(8,128)(2,1)} %collective-permute-done.7, bf16[8,512,64]{1,2,0:T(8,128)(2,1)} %collective-permute-done.6, bf16[8,512,64]{1,2,0:T(8,128)(2,1)} %collective-permute-done.5, bf16[8,512,64]{1,2,0:T(8,128)(2,1)} %copy.95, f32[8,512,2048]{2,1,0:T(8,128)} %get-tuple-element.32, ...), kind=kOutput, calls=%fused_computation.73 | convolution fusion | flops 1107558400 | bytes 36732928 | tf_op jit(solution)/shard_map/hast,hatd->hasd/dot_general | solution.py:14
  332.7 4.8 reshape.829
  342.8 25.0 %multiply_reduce_fusion = (f32[8,1024]{1,0:T(8,128)S(1)}, f32[8,1024,2048]{2,1,0:T(8,128)}) fusion(bf16[8,1024,64]{1,2,0:T(8,128)(2,1)S(1)} %bitcast.141, bf16[8,1024,64]{1,2,0:T(8,128)(2,1)} %collective-permute-done, bf16[8,1024,64]{1,2,0:T(8,128)(2,1)} %bitcast.12), kind=kOutput, calls=%fused_computation.1 | convolution fusion | flops 2185224192 | bytes 70287360 | tf_op jit(solution)/shard_map/hasd,hatd->hast/dot_general | solution.py:10
  367.8 21.3 %fusion = f32[8,1024]{1,0:T(8,128)S(1)} fusion(f32[8,1024,2048]{2,1,0:T(8,128)} %get-tuple-element.34, f32[8,1024]{1,0:T(8,128)S(1)} %get-tuple-element.33), kind=kLoop, calls=%fused_computation.2 | loop fusion | flops 50323456 | bytes 67174400 | tf_op jit(solution)/shard_map/reduce_sum | solution.py:13
  389.9 25.4 %fusion.47 = f32[8,1024,64]{1,2,0:T(8,128)} fusion(bf16[8,1024,64]{1,2,0:T(8,128)(2,1)} %collective-permute-done.1, bf16[8,1024,64]{1,2,0:T(8,128)(2,1)S(1)} %bitcast.145, f32[8,1024,2048]{2,1,0:T(8,128)} %get-tuple-element.34, f32[8,1024]{1,0:T(8,128)S(1)} %get-tuple-element.33, f32[8,1024]{1,0:T(8,128)S(1)} %fusion), kind=kOutput, calls=%fused_computation.70 | convolution fusion | flops 2202533888 | bytes 71368704 | tf_op jit(solution)/shard_map/hast,hatd->hasd/dot_general | solution.py:14
  415.3 4.2 fusion.46
  422.8 57.6 %reduce-scatter.2.cloned.1.call-done = f32[1024,512]{1,0:T(8,128)} async-done(((f32[1024,1024]{1,0:T(8,128)}), f32[1024,512]{1,0:T(8,128)}) %reduce-scatter.2.cloned.1.call-update) | async-done | bytes 2097168 | tf_op jit(solution)/shard_map/reduce_scatter | solution.py:84
  (256 shorter events, 204.3 us)
Async XLA Ops:
  6.5 473.8 %reduce-scatter.2.cloned.1.call-start = ((), (), s32[]{:S(2)}) async-start(), calls=%async_computation.1 | async-start | bytes 6291456 | tf_op jit(solution)/shard_map/reduce_scatter | solution.py:84
  40.2 112.8 %collective-permute-start.37 = (bf16[8,128,64]{1,2,0:T(8,128)(2,1)}, bf16[8,128,64]{1,2,0:T(8,128)(2,1)}, u32[]{:S(2)}, u32[]{:S(2)}) collective-permute-start(bf16[8,128,64]{1,2,0:T(8,128)(2,1)} %copy.131), channel_id=1, source_target_pairs={{0,1},{1,2},{2,3},{3,4},{4,5},{5,6},{6,7},{7,8},{8,9},{9,10},{10,1... | collective-permute-start | bytes 393224 | tf_op jit(solution)/shard_map/ppermute | solution.py:63
  42.2 113.7 %collective-permute-start.38 = (bf16[8,128,64]{1,2,0:T(8,128)(2,1)}, bf16[8,128,64]{1,2,0:T(8,128)(2,1)}, u32[]{:S(2)}, u32[]{:S(2)}) collective-permute-start(bf16[8,128,64]{1,2,0:T(8,128)(2,1)} %copy.131), channel_id=1, source_target_pairs={{0,2},{1,3},{2,4},{3,5},{4,6},{5,7},{6,8},{7,9},{8,10},{9,11},{10,... | collective-permute-start | bytes 393224 | tf_op jit(solution)/shard_map/ppermute | solution.py:63
  44.7 114.9 %collective-permute-start.39 = (bf16[8,128,64]{1,2,0:T(8,128)(2,1)}, bf16[8,128,64]{1,2,0:T(8,128)(2,1)}, u32[]{:S(2)}, u32[]{:S(2)}) collective-permute-start(bf16[8,128,64]{1,2,0:T(8,128)(2,1)} %copy.131), channel_id=1, source_target_pairs={{0,3},{1,4},{2,5},{3,6},{4,7},{5,8},{6,9},{7,10},{8,11},{9,12},{10... | collective-permute-start | bytes 393224 | tf_op jit(solution)/shard_map/ppermute | solution.py:63
  47.7 46.5 %collective-permute-start.22 = (bf16[8,128,64]{1,2,0:T(8,128)(2,1)}, bf16[8,128,64]{1,2,0:T(8,128)(2,1)}, u32[]{:S(2)}, u32[]{:S(2)}) collective-permute-start(bf16[8,128,64]{1,2,0:T(8,128)(2,1)} %copy.125), channel_id=1, source_target_pairs={{0,1},{1,2},{2,3},{3,4},{4,5},{5,6},{6,7},{7,8},{8,9},{9,10},{10,1... | collective-permute-start | bytes 393224 | tf_op jit(solution)/shard_map/ppermute | solution.py:62
  48.0 49.4 %collective-permute-start.23 = (bf16[8,128,64]{1,2,0:T(8,128)(2,1)}, bf16[8,128,64]{1,2,0:T(8,128)(2,1)}, u32[]{:S(2)}, u32[]{:S(2)}) collective-permute-start(bf16[8,128,64]{1,2,0:T(8,128)(2,1)} %copy.125), channel_id=1, source_target_pairs={{0,2},{1,3},{2,4},{3,5},{4,6},{5,7},{6,8},{7,9},{8,10},{9,11},{10,... | collective-permute-start | bytes 393224 | tf_op jit(solution)/shard_map/ppermute | solution.py:62
  147.8 17.8 %collective-permute-start.40 = (bf16[8,128,64]{1,2,0:T(8,128)(2,1)}, bf16[8,128,64]{1,2,0:T(8,128)(2,1)S(1)}, u32[]{:S(2)}, u32[]{:S(2)}) collective-permute-start(bf16[8,128,64]{1,2,0:T(8,128)(2,1)} %copy.131), channel_id=1, source_target_pairs={{0,4},{1,5},{2,6},{3,7},{4,8},{5,9},{6,10},{7,11},{8,12},{9,13},{1... | collective-permute-start | bytes 393224 | tf_op jit(solution)/shard_map/ppermute | solution.py:63
  149.8 15.9 %collective-permute-start.41 = (bf16[8,128,64]{1,2,0:T(8,128)(2,1)}, bf16[8,128,64]{1,2,0:T(8,128)(2,1)S(1)}, u32[]{:S(2)}, u32[]{:S(2)}) collective-permute-start(bf16[8,128,64]{1,2,0:T(8,128)(2,1)} %copy.131), channel_id=1, source_target_pairs={{0,5},{1,6},{2,7},{3,8},{4,9},{5,10},{6,11},{7,12},{8,13},{9,14},{... | collective-permute-start | bytes 393224 | tf_op jit(solution)/shard_map/ppermute | solution.py:63
  177.5 57.9 %collective-permute-start.15 = (bf16[8,256,64]{1,2,0:T(8,128)(2,1)S(1)}, bf16[8,256,64]{1,2,0:T(8,128)(2,1)}, u32[]{:S(2)}, u32[]{:S(2)}) collective-permute-start(bf16[8,256,64]{1,2,0:T(8,128)(2,1)S(1)} %copy-done.10), channel_id=1, source_target_pairs={{0,1},{1,2},{2,3},{3,4},{4,5},{5,6},{6,7},{7,0},{8,9},{9,10},{10,1... | collective-permute-start | bytes 786440 | tf_op jit(solution)/shard_map/ppermute | solution.py:63
  177.8 59.7 %collective-permute-start.16 = (bf16[8,256,64]{1,2,0:T(8,128)(2,1)S(1)}, bf16[8,256,64]{1,2,0:T(8,128)(2,1)}, u32[]{:S(2)}, u32[]{:S(2)}) collective-permute-start(bf16[8,256,64]{1,2,0:T(8,128)(2,1)S(1)} %copy-done.10), channel_id=1, source_target_pairs={{0,2},{1,3},{2,4},{3,5},{4,6},{5,7},{6,0},{7,1},{8,10},{9,11},{10,... | collective-permute-start | bytes 786440 | tf_op jit(solution)/shard_map/ppermute | solution.py:63
  182.5 17.7 %collective-permute-start.8 = (bf16[8,256,64]{1,2,0:T(8,128)(2,1)S(1)}, bf16[8,256,64]{1,2,0:T(8,128)(2,1)}, u32[]{:S(2)}, u32[]{:S(2)}) collective-permute-start(bf16[8,256,64]{1,2,0:T(8,128)(2,1)S(1)} %copy-done.12), channel_id=1, source_target_pairs={{0,1},{1,2},{2,3},{3,4},{4,5},{5,6},{6,7},{7,0},{8,9},{9,10},{10,1... | collective-permute-start | bytes 786440 | tf_op jit(solution)/shard_map/ppermute | solution.py:62
  182.7 19.4 %collective-permute-start.9 = (bf16[8,256,64]{1,2,0:T(8,128)(2,1)S(1)}, bf16[8,256,64]{1,2,0:T(8,128)(2,1)}, u32[]{:S(2)}, u32[]{:S(2)}) collective-permute-start(bf16[8,256,64]{1,2,0:T(8,128)(2,1)S(1)} %copy-done.12), channel_id=1, source_target_pairs={{0,2},{1,3},{2,4},{3,5},{4,6},{5,7},{6,0},{7,1},{8,10},{9,11},{10,... | collective-permute-start | bytes 786440 | tf_op jit(solution)/shard_map/ppermute | solution.py:62
  182.9 22.7 %collective-permute-start.10 = (bf16[8,256,64]{1,2,0:T(8,128)(2,1)S(1)}, bf16[8,256,64]{1,2,0:T(8,128)(2,1)}, u32[]{:S(2)}, u32[]{:S(2)}) collective-permute-start(bf16[8,256,64]{1,2,0:T(8,128)(2,1)S(1)} %copy-done.12), channel_id=1, source_target_pairs={{0,3},{1,4},{2,5},{3,6},{4,7},{5,0},{6,1},{7,2},{8,11},{9,12},{10,... | collective-permute-start | bytes 786440 | tf_op jit(solution)/shard_map/ppermute | solution.py:62
  212.8 28.4 %collective-permute-start.17 = (bf16[8,256,64]{1,2,0:T(8,128)(2,1)S(1)}, bf16[8,256,64]{1,2,0:T(8,128)(2,1)S(1)}, u32[]{:S(2)}, u32[]{:S(2)}) collective-permute-start(bf16[8,256,64]{1,2,0:T(8,128)(2,1)S(1)} %copy-done.10), channel_id=1, source_target_pairs={{0,3},{1,4},{2,5},{3,6},{4,7},{5,0},{6,1},{7,2},{8,11},{9,12},{10,... | collective-permute-start | bytes 786440 | tf_op jit(solution)/shard_map/ppermute | solution.py:63
  218.2 24.6 %collective-permute-start.18 = (bf16[8,256,64]{1,2,0:T(8,128)(2,1)S(1)}, bf16[8,256,64]{1,2,0:T(8,128)(2,1)S(1)}, u32[]{:S(2)}, u32[]{:S(2)}) collective-permute-start(bf16[8,256,64]{1,2,0:T(8,128)(2,1)S(1)} %copy-done.10), channel_id=1, source_target_pairs={{0,4},{1,5},{2,6},{3,7},{4,0},{5,1},{6,2},{7,3},{8,12},{9,13},{10,... | collective-permute-start | bytes 786440 | tf_op jit(solution)/shard_map/ppermute | solution.py:63
  220.9 23.1 %collective-permute-start.19 = (bf16[8,256,64]{1,2,0:T(8,128)(2,1)S(1)}, bf16[8,256,64]{1,2,0:T(8,128)(2,1)S(1)}, u32[]{:S(2)}, u32[]{:S(2)}) collective-permute-start(bf16[8,256,64]{1,2,0:T(8,128)(2,1)S(1)} %copy-done.10), channel_id=1, source_target_pairs={{0,5},{1,6},{2,7},{3,0},{4,1},{5,2},{6,3},{7,4},{8,13},{9,14},{10,... | collective-permute-start | bytes 786440 | tf_op jit(solution)/shard_map/ppermute | solution.py:63
  241.1 71.3 %collective-permute-start.7 = (bf16[8,512,64]{1,2,0:T(8,128)(2,1)}, bf16[8,512,64]{1,2,0:T(8,128)(2,1)}, u32[]{:S(2)}, u32[]{:S(2)}) collective-permute-start(bf16[8,512,64]{1,2,0:T(8,128)(2,1)} %copy.95), channel_id=1, source_target_pairs={{0,3},{1,0},{2,1},{3,2},{4,7},{5,4},{6,5},{7,6},{8,11},{9,8},{10,9... | collective-permute-start | bytes 1572872 | tf_op jit(solution)/shard_map/ppermute | solution.py:63
  242.8 69.7 %collective-permute-start.6 = (bf16[8,512,64]{1,2,0:T(8,128)(2,1)}, bf16[8,512,64]{1,2,0:T(8,128)(2,1)}, u32[]{:S(2)}, u32[]{:S(2)}) collective-permute-start(bf16[8,512,64]{1,2,0:T(8,128)(2,1)} %copy.95), channel_id=1, source_target_pairs={{0,2},{1,3},{2,0},{3,1},{4,6},{5,7},{6,4},{7,5},{8,10},{9,11},{10,... | collective-permute-start | bytes 1572872 | tf_op jit(solution)/shard_map/ppermute | solution.py:63
  244.0 29.9 %collective-permute-start.4 = (bf16[8,512,64]{1,2,0:T(8,128)(2,1)}, bf16[8,512,64]{1,2,0:T(8,128)(2,1)}, u32[]{:S(2)}, u32[]{:S(2)}) collective-permute-start(bf16[8,512,64]{1,2,0:T(8,128)(2,1)} %copy.89), channel_id=1, source_target_pairs={{0,3},{1,0},{2,1},{3,2},{4,7},{5,4},{6,5},{7,6},{8,11},{9,8},{10,9... | collective-permute-start | bytes 1572872 | tf_op jit(solution)/shard_map/ppermute | solution.py:62
  247.3 27.5 %collective-permute-start.3 = (bf16[8,512,64]{1,2,0:T(8,128)(2,1)}, bf16[8,512,64]{1,2,0:T(8,128)(2,1)}, u32[]{:S(2)}, u32[]{:S(2)}) collective-permute-start(bf16[8,512,64]{1,2,0:T(8,128)(2,1)} %copy.89), channel_id=1, source_target_pairs={{0,2},{1,3},{2,0},{3,1},{4,6},{5,7},{6,4},{7,5},{8,10},{9,11},{10,... | collective-permute-start | bytes 1572872 | tf_op jit(solution)/shard_map/ppermute | solution.py:62
  248.1 35.6 %collective-permute-start.2 = (bf16[8,512,64]{1,2,0:T(8,128)(2,1)}, bf16[8,512,64]{1,2,0:T(8,128)(2,1)}, u32[]{:S(2)}, u32[]{:S(2)}) collective-permute-start(bf16[8,512,64]{1,2,0:T(8,128)(2,1)} %copy.89), channel_id=1, source_target_pairs={{0,1},{1,2},{2,3},{3,0},{4,5},{5,6},{6,7},{7,4},{8,9},{9,10},{10,1... | collective-permute-start | bytes 1572872 | tf_op jit(solution)/shard_map/ppermute | solution.py:62
  273.9 38.6 %collective-permute-start.5 = (bf16[8,512,64]{1,2,0:T(8,128)(2,1)}, bf16[8,512,64]{1,2,0:T(8,128)(2,1)}, u32[]{:S(2)}, u32[]{:S(2)}) collective-permute-start(bf16[8,512,64]{1,2,0:T(8,128)(2,1)} %copy.95), channel_id=1, source_target_pairs={{0,1},{1,2},{2,3},{3,0},{4,5},{5,6},{6,7},{7,4},{8,9},{9,10},{10,1... | collective-permute-start | bytes 1572872 | tf_op jit(solution)/shard_map/ppermute | solution.py:63
  274.8 115.1 %collective-permute-start.1 = (bf16[8,1024,64]{1,2,0:T(8,128)(2,1)}, bf16[8,1024,64]{1,2,0:T(8,128)(2,1)}, u32[]{:S(2)}, u32[]{:S(2)}) collective-permute-start(bf16[8,1024,64]{1,2,0:T(8,128)(2,1)} %bitcast.144), channel_id=1, source_target_pairs={{0,1},{1,0},{2,3},{3,2},{4,5},{5,4},{6,7},{7,6},{8,9},{9,8},{10,11... | collective-permute-start | bytes 3145736 | tf_op jit(solution)/shard_map/ppermute | solution.py:63
  283.7 59.1 %collective-permute-start = (bf16[8,1024,64]{1,2,0:T(8,128)(2,1)}, bf16[8,1024,64]{1,2,0:T(8,128)(2,1)}, u32[]{:S(2)}, u32[]{:S(2)}) collective-permute-start(bf16[8,1024,64]{1,2,0:T(8,128)(2,1)} %bitcast.12), channel_id=1, source_target_pairs={{0,1},{1,0},{2,3},{3,2},{4,5},{5,4},{6,7},{7,6},{8,9},{9,8},{10,11... | collective-permute-start | bytes 3145736 | tf_op jit(solution)/shard_map/ppermute | solution.py:62
  (50 other events, 527.3 us)
Sparse Core Ops, SparseCore 0:
  422.9 57.4 reduce-scatter.1
where the time goes:
time: 496 us; the launch traced here: 490 us
  matrix products  110 us (22%)
  local copies, waits for them, and re-layouts  99.5 us (20%)
  starting transfers between devices  99.4 us (20%)
  waiting for transfers between devices  87.7 us (18%)
  other arithmetic  78.7 us (16%)
  between operations  14.4 us (3%)
    reduce_scatter x1, waiting for transfers between devices, device_fn(): reduced = lax.psum_scatter(part_out, 'tp', scatter_dimension=1, tiled=True)  57.6 us
    ppermute x26, starting transfers between devices, device_fn(): k_parts.append(lax.ppermute(k_sel, 'sp', pairs_list))  52.1 us
    dot_general x4, matrix products, attend(): jnp.einsum('hast,hatd->hasd', weights.astype(jnp.bfloat16), v_sel, prefer...  51.5 us
    ppermute x26, starting transfers between devices, device_fn(): v_parts.append(lax.ppermute(v_sel, 'sp', pairs_list))  47.3 us
    dot_general x4, matrix products, attend(): jnp.einsum('hasd,hatd->hast', q_sel, k_sel, preferred_element_type=jnp.fl...  45.1 us
    reduce_sum x4, other arithmetic, attend(): row_sum = jnp.sum(weights, axis=-1, keepdims=True)  40.3 us
    unnamed x86, local copies, waits for them, and re-layouts  27.6 us
    ppermute x26, waiting for transfers between devices, device_fn(): k_parts.append(lax.ppermute(k_sel, 'sp', pairs_list))  26.6 us
  transfers between devices with their start and end apart: 53, of which 14 were waited for; matrix products, arithmetic and copies ran while one was open for 44% of the time, Pallas kernels for 0%

commit v1 on v0

v1 whole, which is shorter than its diff:
```python
import functools

import jax
import jax.numpy as jnp
from jax import lax
from jax.experimental import pallas as pl
from jax.experimental.pallas import tpu as pltpu
from jax.sharding import PartitionSpec as P

MESH = pl.DeviceIdType.MESH
F32 = jnp.float32
BF16 = jnp.bfloat16
ORDER = (0, 4, 2, 6, 1, 5, 3, 7)
HEADS = 8
ROWS = 1024
TILE = 256
KEYS = 2048

UNITS = (
    (0, 0, 0, 256),
    (0, 0, 256, 256),
    (2, -1, 0, 256),
    (0, 0, 512, 256),
    (0, 0, 768, 256),
    (1, 0, 0, 256),
    (1, 0, 256, 256),
    (3, -1, 0, 128),
)


def nt_dot(a, b):
    return lax.dot_general(a, b, (((1,), (1,)), ((), ())), preferred_element_type=F32)


def nn_dot(a, b):
    return jnp.dot(a, b, preferred_element_type=F32)


def kernel(hid, wq, wk, wv, wo, bias, out, hid_v, wq_v, wk_v, wv_v, wo_v, wo_x, xp, q_s, own, r1, r2, r3, r4, s0, s1, p0_s, p1_s,
           m0, m1, l0, l1, num, den, top, o_own, o_oth, outp, in_sem, ssem, rsem, osend, orecv):
    tp = lax.axis_index('tp')
    sp = lax.axis_index('sp')
    x = sp % 4
    y = (sp // 4) % 4
    peers = (sp + 1 - 2 * (x % 2), sp + 3 - 2 * x, sp + 4 * (1 - 2 * (y % 2)), sp + 4 * (3 - 2 * y))

    loads = [pltpu.make_async_copy(a, b, in_sem.at[n]) for n, (a, b) in enumerate(((hid, hid_v), (wk, wk_v), (wv, wv_v), (wq, wq_v), (wo, wo_v)))]
    for load in loads:
        load.start()

    barrier = pltpu.get_barrier_semaphore()
    for peer in peers:
        pl.semaphore_signal(barrier, inc=1, device_id={'sp': peer}, device_id_type=MESH)
    pl.semaphore_signal(barrier, inc=1, device_id={'tp': 1 - tp}, device_id_type=MESH)

    def refs(n, h):
        if n == 0:
            return own.at[h, pl.ds(0, 512)], r1.at[h, pl.ds(0, 512)], 0
        if n == 1:
            return own.at[h, pl.ds(512, 512)], r1.at[h, pl.ds(512, 512)], 0
        if n == 2:
            return own.at[h, pl.ds(0, 512)], r2.at[h, pl.ds(0, 512)], 1
        if n == 3:
            return r1.at[h, pl.ds(0, 512)], r2.at[h, pl.ds(512, 512)], 1
        if n < 8:
            src = (own.at[h, pl.ds(0, 256)], r1.at[h, pl.ds(0, 256)], r2.at[h, pl.ds(0, 256)], r2.at[h, pl.ds(512, 256)])[n - 4]
            return src, r3.at[h, pl.ds((n - 4) * 256, 256)], 2
        if n < 12:
            src = (own.at[h, pl.ds(0, 128)], r1.at[h, pl.ds(0, 128)], r2.at[h, pl.ds(0, 128)], r2.at[h, pl.ds(512, 128)])[n - 8]
        else:
            src = r3.at[h, pl.ds((n - 12) * 256, 128)]
        return src, r4.at[h, pl.ds((n - 8) * 128, 128)], 3

    def copy(n, h):
        src, dst, level = refs(n, h)
        return pltpu.make_async_remote_copy(src, dst, ssem.at[h, n], rsem.at[h, n], device_id={'sp': peers[level]}, device_id_type=MESH)

    def start(h, *chunks):
        for n in chunks:
            copy(n, h).start()

    def arrive(h, *chunks):
        for n in chunks:
            copy(n, h).wait_recv()

    def event1(h):
        arrive(h, 0)
        start(h, 3, 5, 9)
        if isinstance(h, int):
            if h + 2 < HEADS:
                start(h + 2, 2, 4, 8)
        else:
            @pl.when(h + 2 < HEADS)
            def _():
                start(h + 2, 2, 4, 8)

    def event2(h):
        arrive(h, 2)
        start(h, 6, 10)

    def event3(h):
        arrive(h, 3)
        start(h, 7, 11)

    def event4(h):
        arrive(h, 4, 5, 6, 7)
        start(h, 12, 13, 14, 15)

    row_id = lax.broadcasted_iota(jnp.int32, (128, 128), 0)
    col_id = lax.broadcasted_iota(jnp.int32, (128, 128), 1)
    gather = jnp.where(col_id == 8 * (row_id % 16) + row_id // 16, 1.0, 0.0).astype(BF16)
    spread = jnp.where(row_id == 8 * (col_id % 16) + col_id // 16, 1.0, 0.0).astype(BF16)

    loads[0].wait()
    for c in range(8):
        part = nn_dot(gather, hid_v[c * 128:(c + 1) * 128, :]).astype(BF16)
        for r in range(8):
            xp[r * 128 + c * 16:r * 128 + (c + 1) * 16, :] = part[r * 16:(r + 1) * 16, :]

    low = lax.broadcasted_iota(jnp.int32, (512, 128), 1) < 64

    def place(dst, h, half, value):
        for j in range(4):
            pos = ORDER.index((half * 4 + j - h) % 8)
            dst[h, pos * 128:(pos + 1) * 128, :] = value[j * 128:(j + 1) * 128, :]

    loads[1].wait()
    loads[2].wait()
    for half in range(2):
        rows = xp[half * 512:(half + 1) * 512, :]
        key = nn_dot(rows, wk_v[...])
        val = nn_dot(rows, wv_v[...])
        for a in range(4):
            kp = key[:, a * 128:(a + 1) * 128]
            vp = pltpu.roll(val[:, a * 128:(a + 1) * 128], 64, 1)
            place(own, 2 * a, half, jnp.where(low, kp, vp).astype(BF16))
            place(own, 2 * a + 1, half, jnp.where(low, vp, kp).astype(BF16))

    pl.semaphore_wait(barrier, 5)
    for h in range(HEADS):
        start(h, 0, 1)
    for h in range(2):
        start(h, 2, 4, 8)
    loads[4].wait()
    send_w = pltpu.make_async_remote_copy(
        wo_v.at[:, pl.ds(pl.multiple_of((1 - tp) * 512, 512), 512)], wo_x, osend.at[4], orecv.at[4],
        device_id={'tp': 1 - tp}, device_id_type=MESH)
    send_w.start()

    loads[3].wait()
    for half in range(2):
        qry = nn_dot(xp[half * 512:(half + 1) * 512, :], wq_v[...]) * 0.125
        for a in range(4):
            qp = qry[:, a * 128:(a + 1) * 128]
            place(q_s, 2 * a, half, jnp.where(low, qp, 0.0).astype(BF16))
            place(q_s, 2 * a + 1, half, jnp.where(low, 0.0, qp).astype(BF16))
    o_own[...] = jnp.zeros_like(o_own)

    def keys(branch, h):
        if branch == 0:
            parts = [own[h], r1[h]]
        elif branch == 1:
            parts = [own[h, 0:512, :], r1[h, 0:512, :], r2[h]]
        elif branch == 2:
            parts = [own[h, 0:256, :], r1[h, 0:256, :], r2[h, 0:256, :], r2[h, 512:768, :], r3[h]]
        else:
            parts = [own[h, 0:128, :], r1[h, 0:128, :], r2[h, 0:128, :], r2[h, 512:640, :]]
            parts += [r3[h, c * 256:c * 256 + 128, :] for c in range(4)] + [r4[h]]
        return jnp.concatenate(parts, axis=0)

    def logits(u, h):
        branch, shift, first, rows = UNITS[u]
        h = h + shift
        dst = (s0, s1)[u % 2]
        dst[0:rows, :] = nt_dot(q_s[h, first:first + rows, :], keys(branch, h))

    def soften(u):
        rows = UNITS[u][3]
        src, dst, mx, sm = (s0, s1)[u % 2], (p0_s, p1_s)[u % 2], (m0, m1)[u % 2], (l0, l1)[u % 2]
        for g in range(rows // 16):
            at = slice(g * 16, (g + 1) * 16)
            s = src[at, :]
            m = jnp.max(s, axis=1, keepdims=True)
            e = jnp.exp(s - m)
            dst[at, :] = e.astype(BF16)
            mx[at, :] = jnp.broadcast_to(m, (16, 128))
            sm[at, :] = jnp.broadcast_to(jnp.sum(e, axis=1, keepdims=True), (16, 128))

    def gain(u, h):
        branch, shift, first, rows = UNITS[u]
        h = h + shift
        src, mx, sm = (p0_s, p1_s)[u % 2], (m0, m1)[u % 2], (l0, l1)[u % 2]
        got = nn_dot(src[0:rows, :], keys(branch, h))
        slot = h % 2
        at = slice(first, first + rows)
        score = mx[0:rows, :] + bias[branch, tp * HEADS + h]
        if branch == 0:
            num[slot, at, :] = got
            den[slot, at, :] = sm[0:rows, :]
            top[slot, at, :] = score
        else:
            old = top[slot, at, :]
            new = jnp.maximum(old, score)
            keep = jnp.exp(old - new)
            take = jnp.exp(score - new)
            num[slot, at, :] = num[slot, at, :] * keep + got * take
            den[slot, at, :] = den[slot, at, :] * keep + sm[0:rows, :] * take
            top[slot, at, :] = new

    lane = lax.broadcasted_iota(jnp.int32, (128, 128), 1)

    def send_o(a):
        return pltpu.make_async_remote_copy(o_own.at[a], o_oth.at[a], osend.at[a], orecv.at[a], device_id={'tp': 1 - tp}, device_id_type=MESH)

    def finish(h):
        a = h // 2
        limit = 128 - 64 * (h % 2)
        for pos in range(8):
            at = pl.ds(pl.multiple_of(((ORDER[pos] + h) % 8) * 128, 128), 128)
            got = num[h % 2, pos * 128:(pos + 1) * 128, :] / den[h % 2, pos * 128:(pos + 1) * 128, :]
            o_own[a, at, :] = jnp.where(lane < limit, got, o_own[a, at, :].astype(F32)).astype(BF16)
        if isinstance(h, int):
            if h % 2 == 1:
                send_o(a).start()
        else:
            @pl.when(h % 2 == 1)
            def _():
                send_o(a).start()

    event1(0)
    event2(0)

    first = [u for u in range(8) if UNITS[u][1] == 0]

    def before(u, h):
        if u == 0:
            arrive(h, 1)
        elif u == 2:
            event4(h - 1)
        elif u == 3:
            event3(h)
        elif u == 5:
            if isinstance(h, int):
                if h + 1 < HEADS:
                    event1(h + 1)
                    event2(h + 1)
            else:
                @pl.when(h + 1 < HEADS)
                def _():
                    event1(h + 1)
                    event2(h + 1)
        elif u == 7:
            arrive(h - 1, *range(8, 16))

    queue = []
    for u in (0, 1):
        before(u, 0)
        logits(u, 0)
        if u == 1:
            soften(0)
    before(3, 0)
    gain(0, 0)
    soften(1)
    gain(1, 0)
    for u in (4, 3):
        logits(u, 0)
    soften(4)
    soften(3)
    gain(4, 0)
    gain(3, 0)
    before(5, 0)
    logits(5, 0)
    logits(6, 0)
    soften(5)
    gain(5, 0)
    soften(6)

    def step(h, carry):
        for u in range(8):
            before(u, h)
            logits(u, h)
            if u == 0:
                gain(6, h - 1)
            else:
                soften(u - 1)
                if u >= 2:
                    gain(u - 2, h)
        soften(7)
        gain(6, h)
        gain(7, h)
        finish(h - 1)
        return carry

    def run(h, carry):
        return step(h, carry)

    def whole(h, carry):
        for u in range(8):
            before(u, h)
            logits(u, h)
            if u >= 1:
                soften(u - 1)
            if u >= 2:
                gain(u - 2, h)
        soften(7)
        gain(6, h)
        gain(7, h)
        finish(h - 1)
        return carry

    gain(6, 0)
    lax.fori_loop(1, HEADS, whole, 0)

    before(2, HEADS)
    logits(2, HEADS)
    soften(2)
    before(7, HEADS)
    logits(7, HEADS)
    gain(2, HEADS)
    soften(7)
    gain(7, HEADS)
    finish(HEADS - 1)

    send_w.wait()
    for a in range(4):
        send_o(a).wait()
    mine = pl.ds(pl.multiple_of(tp * 512, 512), 512)

    def swapped(ref, cols):
        parts = []
        for a in range(4):
            parts += [ref[a * 128 + 64:a * 128 + 128, cols], ref[a * 128:a * 128 + 64, cols]]
        return parts

    w_all = jnp.concatenate(swapped(wo_v, mine) + swapped(wo_x, slice(None)), axis=0)
    for half in range(2):
        at = slice(half * 512, (half + 1) * 512)
        o_all = jnp.concatenate([o_own[a, at, :] for a in range(4)] + [o_oth[a, at, :] for a in range(4)], axis=1)
        outp[at, :] = nn_dot(o_all, w_all).astype(BF16)
    for c in range(8):
        part = jnp.concatenate([outp[r * 128 + c * 16:r * 128 + (c + 1) * 16, :] for r in range(8)], axis=0)
        out[c * 128:(c + 1) * 128, :] = nn_dot(spread, part).astype(BF16)

    def drain(h, carry):
        for n in range(16):
            copy(n, h).wait_send()
        return carry

    lax.fori_loop(0, HEADS, drain, 0)


def solution(mesh):
    def device_fn(hidden, w_query, w_key, w_value, w_out, branch_bias):
        kv = pltpu.VMEM((HEADS, ROWS, 128), BF16)
        return pl.pallas_call(
            kernel,
            out_shape=jax.ShapeDtypeStruct((ROWS, 512), BF16),
            in_specs=[pl.BlockSpec(memory_space=pl.ANY)] * 5 + [pl.BlockSpec(memory_space=pltpu.SMEM)],
            out_specs=pl.BlockSpec(memory_space=pltpu.VMEM),
            scratch_shapes=[
                pltpu.VMEM((ROWS, 1024), BF16),
                pltpu.VMEM((1024, 512), BF16), pltpu.VMEM((1024, 512), BF16), pltpu.VMEM((1024, 512), BF16),
                pltpu.VMEM((512, 1024), BF16), pltpu.VMEM((512, 512), BF16),
                pltpu.VMEM((ROWS, 1024), BF16),
                kv, kv, kv, kv, kv, kv,
                pltpu.VMEM((TILE, KEYS), F32), pltpu.VMEM((TILE, KEYS), F32),
                pltpu.VMEM((TILE, KEYS), BF16), pltpu.VMEM((TILE, KEYS), BF16),
                pltpu.VMEM((TILE, 128), F32), pltpu.VMEM((TILE, 128), F32),
                pltpu.VMEM((TILE, 128), F32), pltpu.VMEM((TILE, 128), F32),
                pltpu.VMEM((2, ROWS, 128), F32), pltpu.VMEM((2, ROWS, 128), F32), pltpu.VMEM((2, ROWS, 128), F32),
                pltpu.VMEM((4, ROWS, 128), BF16), pltpu.VMEM((4, ROWS, 128), BF16),
                pltpu.VMEM((ROWS, 512), BF16),
                pltpu.SemaphoreType.DMA((5,)),
                pltpu.SemaphoreType.DMA((HEADS, 16)), pltpu.SemaphoreType.DMA((HEADS, 16)),
                pltpu.SemaphoreType.DMA((5,)), pltpu.SemaphoreType.DMA((5,)),
            ],
            compiler_params=pltpu.CompilerParams(collective_id=0, has_side_effects=True, vmem_limit_bytes=62 * 1024 * 1024),
            name='dilated',
        )(hidden, w_query, w_key, w_value, w_out, branch_bias)

    return jax.shard_map(device_fn, mesh=mesh, in_specs=(P(('dp', 'sp'), None), P(None, 'tp'), P(None, 'tp'), P(None, 'tp'), P('tp', None), P(None, None)), out_specs=P(('dp', 'sp'), 'tp'), check_vma=False)
```

time: 496 us -> 91.7 us (0.18); the launches traced: 490 us -> 91.5 us
  matrix products: 110 us -> 0 us
  starting transfers between devices: 99.4 us -> 0 us
  local copies, waits for them, and re-layouts: 99.5 us -> 2.26 us
  Pallas kernels: 0 us -> 89.2 us
  waiting for transfers between devices: 87.7 us -> 0 us
  other arithmetic: 78.7 us -> 0 us
  between operations: 14.4 us -> 0.01 us
    dot_general x12 -> x0, matrix products: 110 us -> none  [the longest x4 51.5 us: attend(): jnp.einsum('hast,hatd->hasd', weights.astype(jnp.bfloat16), v_sel, prefer...]
    ppermute x52 -> x0, starting transfers between devices: 99.4 us -> none  [the longest x26 52.1 us: device_fn(): k_parts.append(lax.ppermute(k_sel, 'sp', pairs_list))]
    pallas_call x0 -> x1, Pallas kernels: none -> 89.2 us  [device_fn(): pl.pallas_call(kernel, out_shape=jax.ShapeDtypeStruct((ROWS, 512), BF16),...]
    reduce_scatter x1 -> x0, waiting for transfers between devices: 57.6 us -> none  [device_fn(): reduced = lax.psum_scatter(part_out, 'tp', scatter_dimension=1, tiled=True)]
    reduce_sum x4 -> x0, other arithmetic: 40.3 us -> none  [attend(): row_sum = jnp.sum(weights, axis=-1, keepdims=True)]
    ppermute x52 -> x0, waiting for transfers between devices: 30.1 us -> none  [the longest x26 26.6 us: device_fn(): k_parts.append(lax.ppermute(k_sel, 'sp', pairs_list))]
    reshape x13 -> x0, local copies, waits for them, and re-layouts: 26.2 us -> none  [the longest x6 22.3 us: device_fn(): jnp.einsum('hsd,hi->sihd', attn_out.reshape(local_heads, kept_rows, head_...]
    unnamed x86 -> x1, local copies, waits for them, and re-layouts: 27.6 us -> 2.26 us
  transfers between devices with their start and end apart: 53 -> 0, of which waited for: 14 -> 0; matrix products, arithmetic and copies ran while one was open for 44% -> 0% of each run, Pallas kernels for 0% -> 0%
where the time goes in v1:
time: 91.7 us; the launch traced here: 91.5 us
  Pallas kernels  89.2 us (97%)
  local copies, waits for them, and re-layouts  2.26 us (2%)
    pallas_call x1, Pallas kernels, device_fn(): pl.pallas_call(kernel, out_shape=jax.ShapeDtypeStruct((ROWS, 512), BF16),...  89.2 us
    unnamed x1, local copies, waits for them, and re-layouts  2.26 us

profile of v1, /device:TPU:1, one launch (start us, length us, event | category | flops | bytes accessed | tf_op | source)
XLA Modules:
  0.0 91.5 jit_solution(5179834998428737574)
XLA Ops:
  0.0 89.2 %dilated.1 = bf16[1024,512]{1,0:T(8,128)(2,1)} custom-call(bf16[1024,1024]{1,0:T(8,128)(2,1)} %hid.1, bf16[1024,512]{1,0:T(8,128)(2,1)} %wq.1, bf16[1024,512]{1,0:T(8,128)(2,1)} %wk.1, bf16[1024,512]{1,0:T(8,128)(2,1)} %wv.1, bf16[512,1024]{1,0:T(8,128)(2,1)} %wo.1, f32[4,16]{1,0:T(4,128)} %bias.1), custom_call_target="tpu_custom_call" | custom-call | tf_op jit(solution)/shard_map/dilated/pallas_call | solution.py:355
  89.2 2.3 %copy.8 = bf16[1024,512]{1,0:T(8,128)(2,1)} copy(bf16[1024,512]{1,0:T(8,128)(2,1)} %dilated.1) | data formatting | bytes 2097152

commit v2 on v1

--- a/solution.py
+++ b/solution.py
@@ -19,12 +19,12 @@
 UNITS = (
     (0, 0, 0, 256),
     (0, 0, 256, 256),
-    (2, -1, 0, 256),
     (0, 0, 512, 256),
     (0, 0, 768, 256),
+    (2, -1, 0, 256),
     (1, 0, 0, 256),
     (1, 0, 256, 256),
-    (3, -1, 0, 128),
+    (3, -2, 0, 128),
 )
 
 
@@ -73,15 +73,22 @@
 
     def copy(n, h):
         src, dst, level = refs(n, h)
-        return pltpu.make_async_remote_copy(src, dst, ssem.at[h, n], rsem.at[h, n], device_id={'sp': peers[level]}, device_id_type=MESH)
+        sem = n if n < 4 else level + 2
+        return pltpu.make_async_remote_copy(src, dst, ssem.at[level], rsem.at[h, sem], device_id={'sp': peers[level]}, device_id_type=MESH)
 
     def start(h, *chunks):
         for n in chunks:
             copy(n, h).start()
 
-    def arrive(h, *chunks):
-        for n in chunks:
-            copy(n, h).wait_recv()
+    def arrive(h, n):
+        copy(n, h).wait_recv()
+
+    def arrive_all(h, level):
+        dst = (r3, r4)[level - 2].at[h]
+        pltpu.make_async_remote_copy(dst, dst, ssem.at[level], rsem.at[h, level + 2], device_id={'sp': peers[level]}, device_id_type=MESH).wait_recv()
+
+    def sent(level):
+        pltpu.make_async_remote_copy(own, own, ssem.at[level], rsem.at[0, 0], device_id={'sp': peers[level]}, device_id_type=MESH).wait_send()
 
     def event1(h):
         arrive(h, 0)
@@ -103,7 +110,7 @@
         start(h, 7, 11)
 
     def event4(h):
-        arrive(h, 4, 5, 6, 7)
+        arrive_all(h, 2)
         start(h, 12, 13, 14, 15)
 
     row_id = lax.broadcasted_iota(jnp.int32, (128, 128), 0)
@@ -124,36 +131,46 @@
             pos = ORDER.index((half * 4 + j - h) % 8)
             dst[h, pos * 128:(pos + 1) * 128, :] = value[j * 128:(j + 1) * 128, :]
 
+    def project_kv(cols):
+        for half in range(2):
+            rows = xp[half * 512:(half + 1) * 512, :]
+            key = nn_dot(rows, wk_v[:, cols * 256:(cols + 1) * 256])
+            val = nn_dot(rows, wv_v[:, cols * 256:(cols + 1) * 256])
+            for a in range(2):
+                h = 4 * cols + 2 * a
+                kp = key[:, a * 128:(a + 1) * 128]
+                vp = pltpu.roll(val[:, a * 128:(a + 1) * 128], 64, 1)
+                place(own, h, half, jnp.where(low, kp, vp).astype(BF16))
+                place(own, h + 1, half, jnp.where(low, vp, kp).astype(BF16))
+
+    def project_q(cols):
+        for half in range(2):
+            qry = nn_dot(xp[half * 512:(half + 1) * 512, :], wq_v[:, cols * 256:(cols + 1) * 256]) * 0.125
+            for a in range(2):
+                h = 4 * cols + 2 * a
+                qp = qry[:, a * 128:(a + 1) * 128]
+                place(q_s, h, half, jnp.where(low, qp, 0.0).astype(BF16))
+                place(q_s, h + 1, half, jnp.where(low, 0.0, qp).astype(BF16))
+
     loads[1].wait()
     loads[2].wait()
-    for half in range(2):
-        rows = xp[half * 512:(half + 1) * 512, :]
-        key = nn_dot(rows, wk_v[...])
-        val = nn_dot(rows, wv_v[...])
-        for a in range(4):
-            kp = key[:, a * 128:(a + 1) * 128]
-            vp = pltpu.roll(val[:, a * 128:(a + 1) * 128], 64, 1)
-            place(own, 2 * a, half, jnp.where(low, kp, vp).astype(BF16))
-            place(own, 2 * a + 1, half, jnp.where(low, vp, kp).astype(BF16))
-
+    project_kv(0)
     pl.semaphore_wait(barrier, 5)
-    for h in range(HEADS):
+    for h in range(2):
+        start(h, 0, 1, 2, 4, 8)
+    for h in range(2, 4):
         start(h, 0, 1)
-    for h in range(2):
-        start(h, 2, 4, 8)
+    project_kv(1)
+    for h in range(4, HEADS):
+        start(h, 0, 1)
     loads[4].wait()
     send_w = pltpu.make_async_remote_copy(
         wo_v.at[:, pl.ds(pl.multiple_of((1 - tp) * 512, 512), 512)], wo_x, osend.at[4], orecv.at[4],
         device_id={'tp': 1 - tp}, device_id_type=MESH)
     send_w.start()
-
     loads[3].wait()
-    for half in range(2):
-        qry = nn_dot(xp[half * 512:(half + 1) * 512, :], wq_v[...]) * 0.125
-        for a in range(4):
-            qp = qry[:, a * 128:(a + 1) * 128]
-            place(q_s, 2 * a, half, jnp.where(low, qp, 0.0).astype(BF16))
-            place(q_s, 2 * a + 1, half, jnp.where(low, 0.0, qp).astype(BF16))
+    project_q(0)
+    project_q(1)
     o_own[...] = jnp.zeros_like(o_own)
 
     def keys(branch, h):
@@ -168,16 +185,13 @@
             parts += [r3[h, c * 256:c * 256 + 128, :] for c in range(4)] + [r4[h]]
         return jnp.concatenate(parts, axis=0)
 
-    def logits(u, h):
-        branch, shift, first, rows = UNITS[u]
-        h = h + shift
-        dst = (s0, s1)[u % 2]
-        dst[0:rows, :] = nt_dot(q_s[h, first:first + rows, :], keys(branch, h))
-
-    def soften(u):
-        rows = UNITS[u][3]
-        src, dst, mx, sm = (s0, s1)[u % 2], (p0_s, p1_s)[u % 2], (m0, m1)[u % 2], (l0, l1)[u % 2]
-        for g in range(rows // 16):
+    def logits(unit, slot):
+        branch, h, first, rows = unit
+        (s0, s1)[slot][0:rows, :] = nt_dot(q_s[h, first:first + rows, :], keys(branch, h))
+
+    def soften(unit, slot):
+        src, dst, mx, sm = (s0, s1)[slot], (p0_s, p1_s)[slot], (m0, m1)[slot], (l0, l1)[slot]
+        for g in range(unit[3] // 16):
             at = slice(g * 16, (g + 1) * 16)
             s = src[at, :]
             m = jnp.max(s, axis=1, keepdims=True)
@@ -186,26 +200,24 @@
             mx[at, :] = jnp.broadcast_to(m, (16, 128))
             sm[at, :] = jnp.broadcast_to(jnp.sum(e, axis=1, keepdims=True), (16, 128))
 
-    def gain(u, h):
-        branch, shift, first, rows = UNITS[u]
-        h = h + shift
-        src, mx, sm = (p0_s, p1_s)[u % 2], (m0, m1)[u % 2], (l0, l1)[u % 2]
+    def gain(unit, slot):
+        branch, h, first, rows = unit
+        src, mx, sm = (p0_s, p1_s)[slot], (m0, m1)[slot], (l0, l1)[slot]
         got = nn_dot(src[0:rows, :], keys(branch, h))
-        slot = h % 2
         at = slice(first, first + rows)
         score = mx[0:rows, :] + bias[branch, tp * HEADS + h]
         if branch == 0:
-            num[slot, at, :] = got
-            den[slot, at, :] = sm[0:rows, :]
-            top[slot, at, :] = score
+            num[h, at, :] = got
+            den[h, at, :] = sm[0:rows, :]
+            top[h, at, :] = score
         else:
-            old = top[slot, at, :]
+            old = top[h, at, :]
             new = jnp.maximum(old, score)
             keep = jnp.exp(old - new)
             take = jnp.exp(score - new)
-            num[slot, at, :] = num[slot, at, :] * keep + got * take
-            den[slot, at, :] = den[slot, at, :] * keep + sm[0:rows, :] * take
-            top[slot, at, :] = new
+            num[h, at, :] = num[h, at, :] * keep + got * take
+            den[h, at, :] = den[h, at, :] * keep + sm[0:rows, :] * take
+            top[h, at, :] = new
 
     lane = lax.broadcasted_iota(jnp.int32, (128, 128), 1)
 
@@ -217,109 +229,80 @@
         limit = 128 - 64 * (h % 2)
         for pos in range(8):
             at = pl.ds(pl.multiple_of(((ORDER[pos] + h) % 8) * 128, 128), 128)
-            got = num[h % 2, pos * 128:(pos + 1) * 128, :] / den[h % 2, pos * 128:(pos + 1) * 128, :]
+            got = num[h, pos * 128:(pos + 1) * 128, :] / den[h, pos * 128:(pos + 1) * 128, :]
             o_own[a, at, :] = jnp.where(lane < limit, got, o_own[a, at, :].astype(F32)).astype(BF16)
-        if isinstance(h, int):
-            if h % 2 == 1:
-                send_o(a).start()
-        else:
-            @pl.when(h % 2 == 1)
-            def _():
-                send_o(a).start()
+
+    def unit_of(u, h):
+        branch, shift, first, rows = UNITS[u]
+        return branch, h + shift, first, rows
+
+    def push(flight, unit):
+        slot = flight[-1][1] ^ 1 if flight else 0
+        logits(unit, slot)
+        if flight:
+            soften(*flight[-1])
+        done = None
+        if len(flight) == 2:
+            gain(*flight[0])
+            done = flight[0][0]
+            flight = flight[1:]
+        return flight + [(unit, slot)], done
+
+    def run(flight, units):
+        for unit in units:
+            flight, done = push(flight, unit)
+            if done is not None and done[0] == 3:
+                finish(done[1])
+        return flight
 
     event1(0)
     event2(0)
-
-    first = [u for u in range(8) if UNITS[u][1] == 0]
-
-    def before(u, h):
-        if u == 0:
-            arrive(h, 1)
-        elif u == 2:
-            event4(h - 1)
-        elif u == 3:
-            event3(h)
-        elif u == 5:
-            if isinstance(h, int):
-                if h + 1 < HEADS:
-                    event1(h + 1)
-                    event2(h + 1)
-            else:
-                @pl.when(h + 1 < HEADS)
-                def _():
-                    event1(h + 1)
-                    event2(h + 1)
-        elif u == 7:
-            arrive(h - 1, *range(8, 16))
-
-    queue = []
-    for u in (0, 1):
-        before(u, 0)
-        logits(u, 0)
-        if u == 1:
-            soften(0)
-    before(3, 0)
-    gain(0, 0)
-    soften(1)
-    gain(1, 0)
-    for u in (4, 3):
-        logits(u, 0)
-    soften(4)
-    soften(3)
-    gain(4, 0)
-    gain(3, 0)
-    before(5, 0)
-    logits(5, 0)
-    logits(6, 0)
-    soften(5)
-    gain(5, 0)
-    soften(6)
-
-    def step(h, carry):
-        for u in range(8):
-            before(u, h)
-            logits(u, h)
-            if u == 0:
-                gain(6, h - 1)
-            else:
-                soften(u - 1)
-                if u >= 2:
-                    gain(u - 2, h)
-        soften(7)
-        gain(6, h)
-        gain(7, h)
-        finish(h - 1)
+    arrive(0, 1)
+    event3(0)
+    event1(1)
+    event2(1)
+    flight = run([], [unit_of(u, 0) for u in (0, 1, 2, 3, 5, 6)])
+    arrive(1, 1)
+    event4(0)
+    event3(1)
+    event1(2)
+    event2(2)
+    flight = run(flight, [unit_of(u, 1) for u in range(7)])
+
+    def body(h, carry):
+        arrive(h, 1)
+        event4(h - 1)
+        event3(h)
+
+        @pl.when(h + 1 < HEADS)
+        def _():
+            event1(h + 1)
+            event2(h + 1)
+
+        @pl.when((h >= 4) & (h % 2 == 0))
+        def _():
+            send_o((h - 4) // 2).start()
+
+        arrive_all(h - 2, 3)
+        units = [unit_of(7, h)] + [unit_of(u, h) for u in range(7)]
+        into = [(unit_of(5, h - 1), flight[0][1]), (unit_of(6, h - 1), flight[1][1])]
+        left = run(into, units)
+        assert [f[1] for f in left] == [f[1] for f in flight]
         return carry
 
-    def run(h, carry):
-        return step(h, carry)
-
-    def whole(h, carry):
-        for u in range(8):
-            before(u, h)
-            logits(u, h)
-            if u >= 1:
-                soften(u - 1)
-            if u >= 2:
-                gain(u - 2, h)
-        soften(7)
-        gain(6, h)
-        gain(7, h)
-        finish(h - 1)
-        return carry
-
-    gain(6, 0)
-    lax.fori_loop(1, HEADS, whole, 0)
-
-    before(2, HEADS)
-    logits(2, HEADS)
-    soften(2)
-    before(7, HEADS)
-    logits(7, HEADS)
-    gain(2, HEADS)
-    soften(7)
-    gain(7, HEADS)
+    lax.fori_loop(2, HEADS, body, 0)
+    flight = [(unit_of(5, HEADS - 1), flight[0][1]), (unit_of(6, HEADS - 1), flight[1][1])]
+    event4(HEADS - 1)
+    send_o(2).start()
+    arrive_all(HEADS - 2, 3)
+    flight = run(flight, [unit_of(7, HEADS), unit_of(4, HEADS)])
+    arrive_all(HEADS - 1, 3)
+    flight = run(flight, [unit_of(7, HEADS + 1)])
+    soften(*flight[1])
+    gain(*flight[0])
+    gain(*flight[1])
     finish(HEADS - 1)
+    send_o(3).start()
 
     send_w.wait()
     for a in range(4):
@@ -341,12 +324,8 @@
         part = jnp.concatenate([outp[r * 128 + c * 16:r * 128 + (c + 1) * 16, :] for r in range(8)], axis=0)
         out[c * 128:(c + 1) * 128, :] = nn_dot(spread, part).astype(BF16)
 
-    def drain(h, carry):
-        for n in range(16):
-            copy(n, h).wait_send()
-        return carry
-
-    lax.fori_loop(0, HEADS, drain, 0)
+    for level in range(4):
+        sent(level)
 
 
 def solution(mesh):
@@ -367,11 +346,11 @@
                 pltpu.VMEM((TILE, KEYS), BF16), pltpu.VMEM((TILE, KEYS), BF16),
                 pltpu.VMEM((TILE, 128), F32), pltpu.VMEM((TILE, 128), F32),
                 pltpu.VMEM((TILE, 128), F32), pltpu.VMEM((TILE, 128), F32),
-                pltpu.VMEM((2, ROWS, 128), F32), pltpu.VMEM((2, ROWS, 128), F32), pltpu.VMEM((2, ROWS, 128), F32),
+                pltpu.VMEM((HEADS, ROWS, 128), F32), pltpu.VMEM((HEADS, ROWS, 128), F32), pltpu.VMEM((HEADS, ROWS, 128), F32),
                 pltpu.VMEM((4, ROWS, 128), BF16), pltpu.VMEM((4, ROWS, 128), BF16),
                 pltpu.VMEM((ROWS, 512), BF16),
                 pltpu.SemaphoreType.DMA((5,)),
-                pltpu.SemaphoreType.DMA((HEADS, 16)), pltpu.SemaphoreType.DMA((HEADS, 16)),
+                pltpu.SemaphoreType.DMA((4,)), pltpu.SemaphoreType.DMA((HEADS, 6)),
                 pltpu.SemaphoreType.DMA((5,)), pltpu.SemaphoreType.DMA((5,)),
             ],
             compiler_params=pltpu.CompilerParams(collective_id=0, has_side_effects=True, vmem_limit_bytes=62 * 1024 * 1024),

time: 91.7 us -> 82.2 us (0.90)
  Pallas kernels: 89.2 us -> 79.8 us
    pallas_call x1, Pallas kernels: 89.2 us -> 79.8 us  [device_fn(): pl.pallas_call(kernel, out_shape=jax.ShapeDtypeStruct((ROWS, 512), BF16),...]
where the time goes in v2:
time: 82.2 us; the launch traced here: 82.1 us
  Pallas kernels  79.8 us (97%)
  local copies, waits for them, and re-layouts  2.26 us (3%)
    pallas_call x1, Pallas kernels, device_fn(): pl.pallas_call(kernel, out_shape=jax.ShapeDtypeStruct((ROWS, 512), BF16),...  79.8 us
    unnamed x1, local copies, waits for them, and re-layouts  2.26 us

profile of v2, /device:TPU:1, one launch (start us, length us, event | category | flops | bytes accessed | tf_op | source)
XLA Modules:
  0.0 82.1 jit_solution(11936008807389996330)
XLA Ops:
  0.0 79.8 %dilated.1 = bf16[1024,512]{1,0:T(8,128)(2,1)} custom-call(bf16[1024,1024]{1,0:T(8,128)(2,1)} %hid.1, bf16[1024,512]{1,0:T(8,128)(2,1)} %wq.1, bf16[1024,512]{1,0:T(8,128)(2,1)} %wk.1, bf16[1024,512]{1,0:T(8,128)(2,1)} %wv.1, bf16[512,1024]{1,0:T(8,128)(2,1)} %wo.1, f32[4,16]{1,0:T(4,128)} %bias.1), custom_call_target="tpu_custom_call" | custom-call | tf_op jit(solution)/shard_map/dilated/pallas_call | solution.py:334
  79.8 2.3 %copy.8 = bf16[1024,512]{1,0:T(8,128)(2,1)} copy(bf16[1024,512]{1,0:T(8,128)(2,1)} %dilated.1) | data formatting | bytes 2097152

commit v3 on v2

v3 whole, which is shorter than its diff:
```python
import functools

import jax
import jax.numpy as jnp
from jax import lax
from jax.experimental import pallas as pl
from jax.experimental.pallas import tpu as pltpu
from jax.sharding import PartitionSpec as P

MESH = pl.DeviceIdType.MESH
F32 = jnp.float32
BF16 = jnp.bfloat16
ORDER = (0, 4, 2, 6, 1, 5, 3, 7)
HEADS = 8
ROWS = 1024
TILE = 256
LANE = 128
HALF = 512
DIM = 64
KEYS = 2048
SLOTS = 2

UNITS = (
    (0, 0, 0, 256),
    (0, 0, 256, 256),
    (0, 0, 512, 256),
    (0, 0, 768, 256),
    (2, -1, 0, 256),
    (1, 0, 0, 256),
    (1, 0, 256, 256),
    (3, -2, 0, 128),
)


def nt_dot(a, b):
    return lax.dot_general(a, b, (((1,), (1,)), ((), ())), preferred_element_type=F32)


def nn_dot(a, b):
    return jnp.dot(a, b, preferred_element_type=F32)


def kernel(hid, wq, wk, wv, wo, bias, out, hid_v, wq_v, wk_v, wv_v, wo_v, wo_x, xp, q_s, own, r1, r2, r3, r4, *more):
    S, PR, M, L = (more[n * SLOTS:(n + 1) * SLOTS] for n in range(4))
    num, den, top, o_own, o_oth, part_o, in_sem, ssem, rsem, osend, orecv = more[4 * SLOTS:]
    tp = lax.axis_index('tp')
    sp = lax.axis_index('sp')
    x = sp % 4
    y = (sp // 4) % 4
    peers = (sp + 1 - 2 * (x % 2), sp + 3 - 2 * x, sp + 4 * (1 - 2 * (y % 2)), sp + 4 * (3 - 2 * y))

    loads = [pltpu.make_async_copy(a, b, in_sem.at[n]) for n, (a, b) in enumerate(((hid, hid_v), (wk, wk_v), (wv, wv_v), (wq, wq_v), (wo, wo_v)))]
    for load in loads:
        load.start()

    barrier = pltpu.get_barrier_semaphore()
    for peer in peers:
        pl.semaphore_signal(barrier, inc=1, device_id={'sp': peer}, device_id_type=MESH)
    pl.semaphore_signal(barrier, inc=1, device_id={'tp': 1 - tp}, device_id_type=MESH)

    def refs(n, h):
        if n == 0:
            return own.at[h, pl.ds(0, HALF)], r1.at[h, pl.ds(0, HALF)], 0
        if n == 1:
            return own.at[h, pl.ds(HALF, HALF)], r1.at[h, pl.ds(HALF, HALF)], 0
        if n == 2:
            return own.at[h, pl.ds(0, HALF)], r2.at[h, pl.ds(0, HALF)], 1
        if n == 3:
            return r1.at[h, pl.ds(0, HALF)], r2.at[h, pl.ds(HALF, HALF)], 1
        if n < 8:
            src = (own.at[h, pl.ds(0, TILE)], r1.at[h, pl.ds(0, TILE)], r2.at[h, pl.ds(0, TILE)], r2.at[h, pl.ds(HALF, TILE)])[n - 4]
            return src, r3.at[h, pl.ds((n - 4) * TILE, TILE)], 2
        if n < 12:
            src = (own.at[h, pl.ds(0, LANE)], r1.at[h, pl.ds(0, LANE)], r2.at[h, pl.ds(0, LANE)], r2.at[h, pl.ds(HALF, LANE)])[n - 8]
        else:
            src = r3.at[h, pl.ds((n - 12) * TILE, LANE)]
        return src, r4.at[h, pl.ds((n - 8) * LANE, LANE)], 3

    def copy(n, h):
        src, dst, level = refs(n, h)
        sem = n if n < 4 else level + 2
        return pltpu.make_async_remote_copy(src, dst, ssem.at[level], rsem.at[h, sem], device_id={'sp': peers[level]}, device_id_type=MESH)

    def start(h, *chunks):
        for n in chunks:
            copy(n, h).start()

    def arrive(h, n):
        copy(n, h).wait_recv()

    def arrive_all(h, level):
        dst = (r3, r4)[level - 2].at[h]
        pltpu.make_async_remote_copy(dst, dst, ssem.at[level], rsem.at[h, level + 2], device_id={'sp': peers[level]}, device_id_type=MESH).wait_recv()

    def sent(level):
        pltpu.make_async_remote_copy(own, own, ssem.at[level], rsem.at[0, 0], device_id={'sp': peers[level]}, device_id_type=MESH).wait_send()

    def event1(h):
        arrive(h, 0)
        start(h, 3, 5, 9)
        if isinstance(h, int):
            if h + 2 < HEADS:
                start(h + 2, 2, 4, 8)
        else:
            @pl.when(h + 2 < HEADS)
            def _():
                start(h + 2, 2, 4, 8)

    def event2(h):
        arrive(h, 2)
        start(h, 6, 10)

    def event3(h):
        arrive(h, 3)
        start(h, 7, 11)

    def event4(h):
        arrive_all(h, 2)
        start(h, 12, 13, 14, 15)

    row_id = lax.broadcasted_iota(jnp.int32, (LANE, LANE), 0)
    col_id = lax.broadcasted_iota(jnp.int32, (LANE, LANE), 1)
    gather = jnp.where(col_id == 8 * (row_id % 16) + row_id // 16, 1.0, 0.0).astype(BF16)

    loads[0].wait()
    for c in range(8):
        part = nn_dot(gather, hid_v[c * LANE:(c + 1) * LANE, :]).astype(BF16)
        for r in range(8):
            xp[r * LANE + c * 16:r * LANE + (c + 1) * 16, :] = part[r * 16:(r + 1) * 16, :]

    low = lax.broadcasted_iota(jnp.int32, (HALF, LANE), 1) < DIM

    def place(dst, h, half, value):
        for j in range(4):
            pos = ORDER.index((half * 4 + j - h) % 8)
            dst[h, pos * LANE:(pos + 1) * LANE, :] = value[j * LANE:(j + 1) * LANE, :]

    def project_kv(cols):
        for half in range(2):
            rows = xp[half * HALF:(half + 1) * HALF, :]
            key = nn_dot(rows, wk_v[:, cols * TILE:(cols + 1) * TILE])
            val = nn_dot(rows, wv_v[:, cols * TILE:(cols + 1) * TILE])
            for a in range(2):
                h = 4 * cols + 2 * a
                kp = key[:, a * LANE:(a + 1) * LANE]
                vp = pltpu.roll(val[:, a * LANE:(a + 1) * LANE], DIM, 1)
                place(own, h, half, jnp.where(low, kp, vp).astype(BF16))
                place(own, h + 1, half, jnp.where(low, vp, kp).astype(BF16))

    def project_q(cols):
        for half in range(2):
            qry = nn_dot(xp[half * HALF:(half + 1) * HALF, :], wq_v[:, cols * TILE:(cols + 1) * TILE]) * 0.125
            for a in range(2):
                h = 4 * cols + 2 * a
                qp = qry[:, a * LANE:(a + 1) * LANE]
                place(q_s, h, half, jnp.where(low, qp, 0.0).astype(BF16))
                place(q_s, h + 1, half, jnp.where(low, 0.0, qp).astype(BF16))

    loads[1].wait()
    loads[2].wait()
    project_kv(0)
    pl.semaphore_wait(barrier, 5)
    for h in range(2):
        start(h, 0, 1, 2, 4, 8)
    for h in range(2, 4):
        start(h, 0, 1)
    project_kv(1)
    for h in range(4, HEADS):
        start(h, 0, 1)
    loads[4].wait()
    send_w = pltpu.make_async_remote_copy(
        wo_v.at[:, pl.ds(pl.multiple_of((1 - tp) * HALF, HALF), HALF)], wo_x, osend.at[4], orecv.at[4],
        device_id={'tp': 1 - tp}, device_id_type=MESH)
    send_w.start()
    loads[3].wait()
    project_q(0)
    project_q(1)
    o_own[...] = jnp.zeros_like(o_own)

    def keys(branch, h):
        if branch == 0:
            parts = [own[h], r1[h]]
        elif branch == 1:
            parts = [own[h, 0:HALF, :], r1[h, 0:HALF, :], r2[h]]
        elif branch == 2:
            parts = [own[h, 0:TILE, :], r1[h, 0:TILE, :], r2[h, 0:TILE, :], r2[h, HALF:768, :], r3[h]]
        else:
            parts = [own[h, 0:LANE, :], r1[h, 0:LANE, :], r2[h, 0:LANE, :], r2[h, HALF:640, :]]
            parts += [r3[h, c * TILE:c * TILE + LANE, :] for c in range(4)] + [r4[h]]
        return jnp.concatenate(parts, axis=0)

    def logits(unit, slot):
        branch, h, first, rows = unit
        s = nt_dot(q_s[h, first:first + rows, :], keys(branch, h))
        S[slot][0:rows, :] = s
        L[slot][0:rows, :] = functools.reduce(jnp.maximum, [s[:, c * LANE:(c + 1) * LANE] for c in range(16)])

    def soften(unit, slot):
        rows = unit[3]
        m = jnp.max(L[slot][0:rows, :], axis=1, keepdims=True)
        e = jnp.exp(S[slot][0:rows, :] - m)
        PR[slot][0:rows, :] = e.astype(BF16)
        M[slot][0:rows, :] = jnp.broadcast_to(m, (rows, LANE))
        L[slot][0:rows, :] = jnp.broadcast_to(jnp.sum(e, axis=1, keepdims=True), (rows, LANE))

    def gain(unit, slot):
        branch, h, first, rows = unit
        src, mx = PR[slot], M[slot]
        sm = L[slot][0:rows, :]
        got = nn_dot(src[0:rows, :], keys(branch, h))
        at = slice(first, first + rows)
        score = mx[0:rows, :] + bias[branch, tp * HEADS + h]
        if branch == 0:
            num[h % 4, at, :] = got
            den[h % 4, at, :] = sm
            top[h % 4, at, :] = score
        else:
            old = top[h % 4, at, :]
            new = jnp.maximum(old, score)
            keep = jnp.exp(old - new)
            take = jnp.exp(score - new)
            num[h % 4, at, :] = num[h % 4, at, :] * keep + got * take
            den[h % 4, at, :] = den[h % 4, at, :] * keep + sm * take
            top[h % 4, at, :] = new

    lane = lax.broadcasted_iota(jnp.int32, (LANE, LANE), 1)

    def send_o(a):
        return pltpu.make_async_remote_copy(o_own.at[a], o_oth.at[a], osend.at[a], orecv.at[a], device_id={'tp': 1 - tp}, device_id_type=MESH)

    def finish(h):
        a = h // 2
        limit = LANE - DIM * (h % 2)
        for pos in range(8):
            at = pl.ds(pl.multiple_of(((ORDER[pos] + h) % 8) * LANE, LANE), LANE)
            got = num[h % 4, pos * LANE:(pos + 1) * LANE, :] / den[h % 4, pos * LANE:(pos + 1) * LANE, :]
            o_own[a, at, :] = jnp.where(lane < limit, got, o_own[a, at, :].astype(F32)).astype(BF16)

    def unit_of(u, h):
        branch, shift, first, rows = UNITS[u]
        return branch, h + shift, first, rows

    def push(flight, unit):
        slot = (flight[-1][1] + 1) % SLOTS if flight else 0
        done = None
        if len(flight) == 2:
            gain(*flight[0])
            done = flight[0][0]
        logits(unit, slot)
        if flight:
            soften(*flight[-1])
        flight = flight[-1:]
        return flight + [(unit, slot)], done

    def run(flight, units):
        for unit in units:
            flight, done = push(flight, unit)
            if done is not None and done[0] == 3:
                finish(done[1])
        return flight

    def each(h, *which):
        return [unit_of(u, h) for u in which]

    event1(0)
    event2(0)
    arrive(0, 1)
    flight = run([], each(0, 0, 1, 2, 3))
    event3(0)
    event1(1)
    event2(1)
    flight = run(flight, each(0, 5, 6))
    arrive(1, 1)
    flight = run(flight, each(1, 0, 1, 2, 3))
    event4(0)
    event3(1)
    event1(2)
    event2(2)
    flight = run(flight, each(1, 4, 5, 6))

    def entering(h):
        return [(unit_of(5, h - 1), flight[0][1]), (unit_of(6, h - 1), flight[1][1])]

    def body(h, carry):
        arrive(h, 1)
        event4(h - 1)
        event3(h)
        event1(h + 1)
        event2(h + 1)

        @pl.when((h >= 4) & (h % 2 == 0))
        def _():
            send_o((h - 4) // 2).start()

        arrive_all(h - 2, 3)
        left = run(entering(h), [unit_of(7, h)] + each(h, 0, 1, 2, 3, 4, 5, 6))
        assert [f[1] for f in left] == [f[1] for f in flight]
        return carry

    lax.fori_loop(2, HEADS - 1, body, 0)
    last = HEADS - 1
    arrive(last, 1)
    event4(last - 1)
    event3(last)
    arrive_all(last - 2, 3)
    flight = run(entering(last), [unit_of(7, last)] + each(last, 0, 1, 2, 3))
    event4(last)
    send_o(2).start()
    flight = run(flight, each(last, 4, 5, 6))
    arrive_all(last - 1, 3)
    flight = run(flight, [unit_of(7, HEADS), unit_of(4, HEADS)])
    arrive_all(last, 3)
    flight = run(flight, [unit_of(7, HEADS + 1)])
    gain(*flight[0])
    soften(*flight[1])
    gain(*flight[1])
    finish(last)
    send_o(3).start()

    mine = pl.ds(pl.multiple_of(tp * HALF, HALF), HALF)

    def swapped(ref, cols):
        parts = []
        for a in range(4):
            parts += [ref[a * LANE + DIM:a * LANE + LANE, cols], ref[a * LANE:a * LANE + DIM, cols]]
        return jnp.concatenate(parts, axis=0)

    def heads_of(ref, half):
        return jnp.concatenate([ref[a, half * HALF:(half + 1) * HALF, :] for a in range(4)], axis=1)

    w_mine = swapped(wo_v, mine)
    for half in range(2):
        part_o[half * HALF:(half + 1) * HALF, :] = nn_dot(heads_of(o_own, half), w_mine)
    send_w.wait()
    for a in range(4):
        send_o(a).wait()
    w_other = swapped(wo_x, slice(None))
    for half in range(2):
        at = slice(half * HALF, (half + 1) * HALF)
        out[at, :] = (part_o[at, :] + nn_dot(heads_of(o_oth, half), w_other)).astype(BF16)
    for level in range(4):
        sent(level)


def restore(outp, out):
    row_id = lax.broadcasted_iota(jnp.int32, (LANE, LANE), 0)
    col_id = lax.broadcasted_iota(jnp.int32, (LANE, LANE), 1)
    spread = jnp.where(row_id == 8 * (col_id % 16) + col_id // 16, 1.0, 0.0).astype(BF16)
    for c in range(8):
        part = jnp.concatenate([outp[r * LANE + c * 16:r * LANE + (c + 1) * 16, :] for r in range(8)], axis=0)
        out[c * LANE:(c + 1) * LANE, :] = nn_dot(spread, part).astype(BF16)


def solution(mesh):
    def device_fn(hidden, w_query, w_key, w_value, w_out, branch_bias):
        kv = pltpu.VMEM((HEADS, ROWS, LANE), BF16)
        permuted = pl.pallas_call(
            kernel,
            out_shape=jax.ShapeDtypeStruct((ROWS, HALF), BF16),
            in_specs=[pl.BlockSpec(memory_space=pl.ANY)] * 5 + [pl.BlockSpec(memory_space=pltpu.SMEM)],
            out_specs=pl.BlockSpec(memory_space=pltpu.VMEM),
            scratch_shapes=[
                pltpu.VMEM((ROWS, 1024), BF16),
                pltpu.VMEM((1024, HALF), BF16), pltpu.VMEM((1024, HALF), BF16), pltpu.VMEM((1024, HALF), BF16),
                pltpu.VMEM((HALF, 1024), BF16), pltpu.VMEM((HALF, HALF), BF16),
                pltpu.VMEM((ROWS, 1024), BF16),
                kv, kv, kv, kv, kv, kv,
                *[pltpu.VMEM((TILE, KEYS), F32)] * SLOTS, *[pltpu.VMEM((TILE, KEYS), BF16)] * SLOTS,
                *[pltpu.VMEM((TILE, LANE), F32)] * (2 * SLOTS),
                pltpu.VMEM((4, ROWS, LANE), F32), pltpu.VMEM((4, ROWS, LANE), F32), pltpu.VMEM((4, ROWS, LANE), F32),
                pltpu.VMEM((4, ROWS, LANE), BF16), pltpu.VMEM((4, ROWS, LANE), BF16),
                pltpu.VMEM((ROWS, HALF), F32),
                pltpu.SemaphoreType.DMA((5,)),
                pltpu.SemaphoreType.DMA((4,)), pltpu.SemaphoreType.DMA((HEADS, 6)),
                pltpu.SemaphoreType.DMA((5,)), pltpu.SemaphoreType.DMA((5,)),
            ],
            compiler_params=pltpu.CompilerParams(collective_id=0, has_side_effects=True, vmem_limit_bytes=62 * 1024 * 1024),
            name='dilated',
        )(hidden, w_query, w_key, w_value, w_out, branch_bias)
        return pl.pallas_call(
            restore,
            out_shape=jax.ShapeDtypeStruct((ROWS, HALF), BF16),
            in_specs=[pl.BlockSpec(memory_space=pltpu.VMEM)],
            out_specs=pl.BlockSpec(memory_space=pltpu.VMEM),
            name='restore',
        )(permuted)

    return jax.shard_map(device_fn, mesh=mesh, in_specs=(P(('dp', 'sp'), None), P(None, 'tp'), P(None, 'tp'), P(None, 'tp'), P('tp', None), P(None, None)), out_specs=P(('dp', 'sp'), 'tp'), check_vma=False)
```

time: 82.2 us -> 77.2 us (0.939)
  Pallas kernels: 79.8 us -> 77.1 us
  local copies, waits for them, and re-layouts: 2.26 us -> 0 us
    pallas_call x1 -> x2, Pallas kernels: 79.8 us -> 77.1 us  [the longest x1 74.5 us: device_fn(): pl.pallas_call(kernel, out_shape=jax.ShapeDtypeStruct((ROWS, HALF), BF16)...]
    unnamed x1 -> x0, local copies, waits for them, and re-layouts: 2.26 us -> none
where the time goes in v3:
time: 77.2 us; the launch traced here: 77.1 us
  Pallas kernels  77.1 us (100%)
    pallas_call x1, Pallas kernels, device_fn(): pl.pallas_call(kernel, out_shape=jax.ShapeDtypeStruct((ROWS, HALF), BF16)...  74.5 us
    pallas_call x1, Pallas kernels, device_fn(): pl.pallas_call(restore, out_shape=jax.ShapeDtypeStruct((ROWS, HALF), BF16...  2.62 us

profile of v3, /device:TPU:1, one launch (start us, length us, event | category | flops | bytes accessed | tf_op | source)
XLA Modules:
  0.0 77.1 jit_solution(10189940268607845298)
XLA Ops:
  0.0 74.5 %dilated.1.outp = bf16[1024,512]{1,0:T(8,128)(2,1)} custom-call(bf16[1024,1024]{1,0:T(8,128)(2,1)} %hid.1, bf16[1024,512]{1,0:T(8,128)(2,1)} %wq.1, bf16[1024,512]{1,0:T(8,128)(2,1)} %wk.1, bf16[1024,512]{1,0:T(8,128)(2,1)} %wv.1, bf16[512,1024]{1,0:T(8,128)(2,1)} %wo.1, f32[4,16]{1,0:T(4,128)} %bias.1), custom_call_target="tpu_custom_call" | custom-call | tf_op jit(solution)/shard_map/dilated/pallas_call | solution.py:357
  74.5 2.6 %restore.1 = bf16[1024,512]{1,0:T(8,128)(2,1)} custom-call(bf16[1024,512]{1,0:T(8,128)(2,1)} %dilated.1.outp), custom_call_target="tpu_custom_call" | custom-call | tf_op jit(solution)/shard_map/restore/pallas_call | solution.py:380

commit v4 on v3

--- a/solution.py
+++ b/solution.py
@@ -15,6 +15,7 @@
 ROWS = 1024
 TILE = 256
 LANE = 128
+SUB = 8
 HALF = 512
 DIM = 64
 KEYS = 2048
@@ -36,13 +37,17 @@
     return lax.dot_general(a, b, (((1,), (1,)), ((), ())), preferred_element_type=F32)
 
 
+def tn_dot(a, b):
+    return lax.dot_general(a, b, (((0,), (0,)), ((), ())), preferred_element_type=F32)
+
+
 def nn_dot(a, b):
     return jnp.dot(a, b, preferred_element_type=F32)
 
 
 def kernel(hid, wq, wk, wv, wo, bias, out, hid_v, wq_v, wk_v, wv_v, wo_v, wo_x, xp, q_s, own, r1, r2, r3, r4, *more):
-    S, PR, M, L = (more[n * SLOTS:(n + 1) * SLOTS] for n in range(4))
-    num, den, top, o_own, o_oth, part_o, in_sem, ssem, rsem, osend, orecv = more[4 * SLOTS:]
+    S, PR, M, L, T = (more[n * SLOTS:(n + 1) * SLOTS] for n in range(5))
+    num, den, top, o_t, o_own, o_oth, part_o, in_sem, ssem, rsem, osend, orecv = more[5 * SLOTS:]
     tp = lax.axis_index('tp')
     sp = lax.axis_index('sp')
     x = sp % 4
@@ -175,7 +180,7 @@
     loads[3].wait()
     project_q(0)
     project_q(1)
-    o_own[...] = jnp.zeros_like(o_own)
+    o_t[...] = jnp.zeros_like(o_t)
 
     def keys(branch, h):
         if branch == 0:
@@ -191,50 +196,55 @@
 
     def logits(unit, slot):
         branch, h, first, rows = unit
-        s = nt_dot(q_s[h, first:first + rows, :], keys(branch, h))
-        S[slot][0:rows, :] = s
-        L[slot][0:rows, :] = functools.reduce(jnp.maximum, [s[:, c * LANE:(c + 1) * LANE] for c in range(16)])
+        s = nt_dot(keys(branch, h), q_s[h, first:first + rows, :])
+        S[slot][:, 0:rows] = s
+        M[slot][:, 0:rows] = jnp.broadcast_to(jnp.max(s, axis=0, keepdims=True), (SUB, rows))
 
     def soften(unit, slot):
         rows = unit[3]
-        m = jnp.max(L[slot][0:rows, :], axis=1, keepdims=True)
-        e = jnp.exp(S[slot][0:rows, :] - m)
-        PR[slot][0:rows, :] = e.astype(BF16)
-        M[slot][0:rows, :] = jnp.broadcast_to(m, (rows, LANE))
-        L[slot][0:rows, :] = jnp.broadcast_to(jnp.sum(e, axis=1, keepdims=True), (rows, LANE))
+        m = M[slot][0:1, 0:rows]
+        total = jnp.zeros((1, rows), F32)
+        for c in range(KEYS // HALF):
+            at = slice(c * HALF, (c + 1) * HALF)
+            e = jnp.exp(S[slot][at, 0:rows] - m)
+            PR[slot][at, 0:rows] = e.astype(BF16)
+            total = total + jnp.sum(e, axis=0, keepdims=True)
+        T[slot][:, 0:rows] = jnp.broadcast_to(m, (SUB, rows))
+        L[slot][:, 0:rows] = jnp.broadcast_to(total, (SUB, rows))
 
     def gain(unit, slot):
         branch, h, first, rows = unit
-        src, mx = PR[slot], M[slot]
-        sm = L[slot][0:rows, :]
-        got = nn_dot(src[0:rows, :], keys(branch, h))
+        got = tn_dot(keys(branch, h), PR[slot][:, 0:rows])
+        total = L[slot][:, 0:rows]
         at = slice(first, first + rows)
-        score = mx[0:rows, :] + bias[branch, tp * HEADS + h]
+        score = T[slot][:, 0:rows] + bias[branch, tp * HEADS + h]
         if branch == 0:
-            num[h % 4, at, :] = got
-            den[h % 4, at, :] = sm
-            top[h % 4, at, :] = score
+            num[h % 4, :, at] = got
+            den[h % 4, :, at] = total
+            top[h % 4, :, at] = score
         else:
-            old = top[h % 4, at, :]
+            old = top[h % 4, :, at]
             new = jnp.maximum(old, score)
             keep = jnp.exp(old - new)
             take = jnp.exp(score - new)
-            num[h % 4, at, :] = num[h % 4, at, :] * keep + got * take
-            den[h % 4, at, :] = den[h % 4, at, :] * keep + sm * take
-            top[h % 4, at, :] = new
-
-    lane = lax.broadcasted_iota(jnp.int32, (LANE, LANE), 1)
+            num[h % 4, :, at] = num[h % 4, :, at] * keep[0:1, :] + got * take[0:1, :]
+            den[h % 4, :, at] = den[h % 4, :, at] * keep + total * take
+            top[h % 4, :, at] = new
 
     def send_o(a):
         return pltpu.make_async_remote_copy(o_own.at[a], o_oth.at[a], osend.at[a], orecv.at[a], device_id={'tp': 1 - tp}, device_id_type=MESH)
 
     def finish(h):
-        a = h // 2
-        limit = LANE - DIM * (h % 2)
+        a, odd = h // 2, h % 2
+        have = pl.ds(pl.multiple_of((1 - odd) * DIM, DIM), DIM)
+        want = pl.ds(pl.multiple_of(odd * DIM, DIM), DIM)
         for pos in range(8):
-            at = pl.ds(pl.multiple_of(((ORDER[pos] + h) % 8) * LANE, LANE), LANE)
-            got = num[h % 4, pos * LANE:(pos + 1) * LANE, :] / den[h % 4, pos * LANE:(pos + 1) * LANE, :]
-            o_own[a, at, :] = jnp.where(lane < limit, got, o_own[a, at, :].astype(F32)).astype(BF16)
+            at = slice(pos * LANE, (pos + 1) * LANE)
+            to = pl.ds(pl.multiple_of(((ORDER[pos] + h) % 8) * LANE, LANE), LANE)
+            o_t[a, want, to] = num[h % 4, have, at] / den[h % 4, 0:1, at]
+        for r in range(8):
+            at = slice(r * LANE, (r + 1) * LANE)
+            o_own[a, at, :] = o_t[a, :, at].T.astype(BF16)
 
     def unit_of(u, h):
         branch, shift, first, rows = UNITS[u]
@@ -242,15 +252,12 @@
 
     def push(flight, unit):
         slot = (flight[-1][1] + 1) % SLOTS if flight else 0
-        done = None
-        if len(flight) == 2:
-            gain(*flight[0])
-            done = flight[0][0]
+        pl.delay(1)
         logits(unit, slot)
         if flight:
             soften(*flight[-1])
-        flight = flight[-1:]
-        return flight + [(unit, slot)], done
+            gain(*flight[-1])
+        return [(unit, slot)], flight[-1][0] if flight else None
 
     def run(flight, units):
         for unit in units:
@@ -279,7 +286,7 @@
     flight = run(flight, each(1, 4, 5, 6))
 
     def entering(h):
-        return [(unit_of(5, h - 1), flight[0][1]), (unit_of(6, h - 1), flight[1][1])]
+        return [(unit_of(6, h - 1), flight[0][1])]
 
     def body(h, carry):
         arrive(h, 1)
@@ -311,30 +318,23 @@
     flight = run(flight, [unit_of(7, HEADS), unit_of(4, HEADS)])
     arrive_all(last, 3)
     flight = run(flight, [unit_of(7, HEADS + 1)])
+    soften(*flight[0])
     gain(*flight[0])
-    soften(*flight[1])
-    gain(*flight[1])
     finish(last)
     send_o(3).start()
 
     mine = pl.ds(pl.multiple_of(tp * HALF, HALF), HALF)
 
-    def swapped(ref, cols):
-        parts = []
-        for a in range(4):
-            parts += [ref[a * LANE + DIM:a * LANE + LANE, cols], ref[a * LANE:a * LANE + DIM, cols]]
-        return jnp.concatenate(parts, axis=0)
-
     def heads_of(ref, half):
         return jnp.concatenate([ref[a, half * HALF:(half + 1) * HALF, :] for a in range(4)], axis=1)
 
-    w_mine = swapped(wo_v, mine)
+    w_mine = wo_v[:, mine]
     for half in range(2):
         part_o[half * HALF:(half + 1) * HALF, :] = nn_dot(heads_of(o_own, half), w_mine)
     send_w.wait()
     for a in range(4):
         send_o(a).wait()
-    w_other = swapped(wo_x, slice(None))
+    w_other = wo_x[...]
     for half in range(2):
         at = slice(half * HALF, (half + 1) * HALF)
         out[at, :] = (part_o[at, :] + nn_dot(heads_of(o_oth, half), w_other)).astype(BF16)
@@ -365,9 +365,9 @@
                 pltpu.VMEM((HALF, 1024), BF16), pltpu.VMEM((HALF, HALF), BF16),
                 pltpu.VMEM((ROWS, 1024), BF16),
                 kv, kv, kv, kv, kv, kv,
-                *[pltpu.VMEM((TILE, KEYS), F32)] * SLOTS, *[pltpu.VMEM((TILE, KEYS), BF16)] * SLOTS,
-                *[pltpu.VMEM((TILE, LANE), F32)] * (2 * SLOTS),
-                pltpu.VMEM((4, ROWS, LANE), F32), pltpu.VMEM((4, ROWS, LANE), F32), pltpu.VMEM((4, ROWS, LANE), F32),
+                *[pltpu.VMEM((KEYS, TILE), F32)] * SLOTS, *[pltpu.VMEM((KEYS, TILE), BF16)] * SLOTS,
+                *[pltpu.VMEM((SUB, TILE), F32)] * (3 * SLOTS),
+                pltpu.VMEM((4, LANE, ROWS), F32), pltpu.VMEM((4, SUB, ROWS), F32), pltpu.VMEM((4, SUB, ROWS), F32), pltpu.VMEM((4, LANE, ROWS), F32),
                 pltpu.VMEM((4, ROWS, LANE), BF16), pltpu.VMEM((4, ROWS, LANE), BF16),
                 pltpu.VMEM((ROWS, HALF), F32),
                 pltpu.SemaphoreType.DMA((5,)),

time: 77.2 us -> 75.7 us (0.981)
  Pallas kernels: 77.1 us -> 75.6 us
    pallas_call x1, Pallas kernels: 74.5 us -> 72.9 us  [device_fn(): pl.pallas_call(kernel, out_shape=jax.ShapeDtypeStruct((ROWS, HALF), BF16)...]
where the time goes in v4:
time: 75.7 us; the launch traced here: 75.6 us
  Pallas kernels  75.6 us (100%)
    pallas_call x1, Pallas kernels, device_fn(): pl.pallas_call(kernel, out_shape=jax.ShapeDtypeStruct((ROWS, HALF), BF16)...  72.9 us
    pallas_call x1, Pallas kernels, device_fn(): pl.pallas_call(restore, out_shape=jax.ShapeDtypeStruct((ROWS, HALF), BF16...  2.62 us

profile of v4, /device:TPU:1, one launch (start us, length us, event | category | flops | bytes accessed | tf_op | source)
XLA Modules:
  0.0 75.6 jit_solution(1032404533439671384)
XLA Ops:
  0.0 72.9 %dilated.1.outp = bf16[1024,512]{1,0:T(8,128)(2,1)} custom-call(bf16[1024,1024]{1,0:T(8,128)(2,1)} %hid.1, bf16[1024,512]{1,0:T(8,128)(2,1)} %wq.1, bf16[1024,512]{1,0:T(8,128)(2,1)} %wk.1, bf16[1024,512]{1,0:T(8,128)(2,1)} %wv.1, bf16[512,1024]{1,0:T(8,128)(2,1)} %wo.1, f32[4,16]{1,0:T(4,128)} %bias.1), custom_call_target="tpu_custom_call" | custom-call | tf_op jit(solution)/shard_map/dilated/pallas_call | solution.py:357
  72.9 2.6 %restore.1 = bf16[1024,512]{1,0:T(8,128)(2,1)} custom-call(bf16[1024,512]{1,0:T(8,128)(2,1)} %dilated.1.outp), custom_call_target="tpu_custom_call" | custom-call | tf_op jit(solution)/shard_map/restore/pallas_call | solution.py:380

commit v5 on v4

--- a/solution.py
+++ b/solution.py
@@ -22,14 +22,14 @@
 SLOTS = 2
 
 UNITS = (
-    (0, 0, 0, 256),
-    (0, 0, 256, 256),
-    (0, 0, 512, 256),
-    (0, 0, 768, 256),
-    (2, -1, 0, 256),
-    (1, 0, 0, 256),
-    (1, 0, 256, 256),
-    (3, -2, 0, 128),
+    (0, 0, 0, TILE),
+    (0, 0, TILE, TILE),
+    (0, 0, 2 * TILE, TILE),
+    (0, 0, 3 * TILE, TILE),
+    (2, -1, 0, TILE),
+    (1, 0, 0, TILE),
+    (1, 0, TILE, TILE),
+    (3, -1, 0, LANE),
 )
 
 
@@ -83,7 +83,7 @@
 
     def copy(n, h):
         src, dst, level = refs(n, h)
-        sem = n if n < 4 else level + 2
+        sem = min(n, 8)
         return pltpu.make_async_remote_copy(src, dst, ssem.at[level], rsem.at[h, sem], device_id={'sp': peers[level]}, device_id_type=MESH)
 
     def start(h, *chunks):
@@ -93,9 +93,8 @@
     def arrive(h, n):
         copy(n, h).wait_recv()
 
-    def arrive_all(h, level):
-        dst = (r3, r4)[level - 2].at[h]
-        pltpu.make_async_remote_copy(dst, dst, ssem.at[level], rsem.at[h, level + 2], device_id={'sp': peers[level]}, device_id_type=MESH).wait_recv()
+    def arrive_all(h):
+        pltpu.make_async_remote_copy(r4.at[h], r4.at[h], ssem.at[3], rsem.at[h, 8], device_id={'sp': peers[3]}, device_id_type=MESH).wait_recv()
 
     def sent(level):
         pltpu.make_async_remote_copy(own, own, ssem.at[level], rsem.at[0, 0], device_id={'sp': peers[level]}, device_id_type=MESH).wait_send()
@@ -119,9 +118,10 @@
         arrive(h, 3)
         start(h, 7, 11)
 
-    def event4(h):
-        arrive_all(h, 2)
-        start(h, 12, 13, 14, 15)
+    def event4(h, *parts):
+        for c in parts:
+            arrive(h, 4 + c)
+            start(h, 12 + c)
 
     row_id = lax.broadcasted_iota(jnp.int32, (LANE, LANE), 0)
     col_id = lax.broadcasted_iota(jnp.int32, (LANE, LANE), 1)
@@ -259,68 +259,61 @@
             gain(*flight[-1])
         return [(unit, slot)], flight[-1][0] if flight else None
 
-    def run(flight, units):
-        for unit in units:
-            flight, done = push(flight, unit)
+    def run(flight, h, *which):
+        for u in which:
+            flight, done = push(flight, unit_of(u, h))
             if done is not None and done[0] == 3:
                 finish(done[1])
         return flight
 
-    def each(h, *which):
-        return [unit_of(u, h) for u in which]
-
     event1(0)
     event2(0)
     arrive(0, 1)
-    flight = run([], each(0, 0, 1, 2, 3))
+    flight = run([], 0, 0)
+    event2(1)
+    flight = run(flight, 0, 1, 2, 3)
     event3(0)
     event1(1)
-    event2(1)
-    flight = run(flight, each(0, 5, 6))
-    arrive(1, 1)
-    flight = run(flight, each(1, 0, 1, 2, 3))
-    event4(0)
-    event3(1)
-    event1(2)
-    event2(2)
-    flight = run(flight, each(1, 4, 5, 6))
-
-    def entering(h):
-        return [(unit_of(6, h - 1), flight[0][1])]
+    event4(0, 0, 1, 2)
+    flight = run(flight, 0, 5, 6)
+
+    def guard(condition, action):
+        if not isinstance(condition, bool):
+            pl.when(condition)(action)
+        elif condition:
+            action()
+
+    def pass_of(h, flight):
+        arrive(h, 1)
+        flight = run(flight, h, 0)
+        guard(h + 1 < HEADS, lambda: event2(h + 1))
+        guard((h >= 3) & (h % 2 == 1), lambda: send_o((h - 3) // 2).start())
+        flight = run(flight, h, 1)
+        event4(h - 1, 3)
+        flight = run(flight, h, 2, 3, 4)
+        event3(h)
+        guard(h + 1 < HEADS, lambda: event1(h + 1))
+        event4(h, 0, 1, 2)
+        flight = run(flight, h, 5, 6)
+        arrive_all(h - 1)
+        return run(flight, h, 7)
+
+    flight = pass_of(1, flight)
 
     def body(h, carry):
-        arrive(h, 1)
-        event4(h - 1)
-        event3(h)
-        event1(h + 1)
-        event2(h + 1)
-
-        @pl.when((h >= 4) & (h % 2 == 0))
-        def _():
-            send_o((h - 4) // 2).start()
-
-        arrive_all(h - 2, 3)
-        left = run(entering(h), [unit_of(7, h)] + each(h, 0, 1, 2, 3, 4, 5, 6))
-        assert [f[1] for f in left] == [f[1] for f in flight]
+        left = pass_of(h, [(unit_of(7, h - 1), flight[0][1])])
+        assert left[0][1] == flight[0][1]
         return carry
 
-    lax.fori_loop(2, HEADS - 1, body, 0)
-    last = HEADS - 1
-    arrive(last, 1)
-    event4(last - 1)
-    event3(last)
-    arrive_all(last - 2, 3)
-    flight = run(entering(last), [unit_of(7, last)] + each(last, 0, 1, 2, 3))
-    event4(last)
-    send_o(2).start()
-    flight = run(flight, each(last, 4, 5, 6))
-    arrive_all(last - 1, 3)
-    flight = run(flight, [unit_of(7, HEADS), unit_of(4, HEADS)])
-    arrive_all(last, 3)
-    flight = run(flight, [unit_of(7, HEADS + 1)])
+    lax.fori_loop(2, HEADS, body, 0)
+    flight = [(unit_of(7, HEADS - 1), flight[0][1])]
+    event4(HEADS - 1, 3)
+    flight = run(flight, HEADS, 4)
+    arrive_all(HEADS - 1)
+    flight = run(flight, HEADS, 7)
     soften(*flight[0])
     gain(*flight[0])
-    finish(last)
+    finish(HEADS - 1)
     send_o(3).start()
 
     mine = pl.ds(pl.multiple_of(tp * HALF, HALF), HALF)
@@ -371,7 +364,7 @@
                 pltpu.VMEM((4, ROWS, LANE), BF16), pltpu.VMEM((4, ROWS, LANE), BF16),
                 pltpu.VMEM((ROWS, HALF), F32),
                 pltpu.SemaphoreType.DMA((5,)),
-                pltpu.SemaphoreType.DMA((4,)), pltpu.SemaphoreType.DMA((HEADS, 6)),
+                pltpu.SemaphoreType.DMA((4,)), pltpu.SemaphoreType.DMA((HEADS, 9)),
                 pltpu.SemaphoreType.DMA((5,)), pltpu.SemaphoreType.DMA((5,)),
             ],
             compiler_params=pltpu.CompilerParams(collective_id=0, has_side_effects=True, vmem_limit_bytes=62 * 1024 * 1024),

time: 75.7 us -> 75.3 us (level)
  no operation moved by 1% of the time
where the time goes in v5:
time: 75.3 us; the launch traced here: 75.1 us
  Pallas kernels  75.1 us (100%)
    pallas_call x1, Pallas kernels, device_fn(): pl.pallas_call(kernel, out_shape=jax.ShapeDtypeStruct((ROWS, HALF), BF16)...  72.5 us
    pallas_call x1, Pallas kernels, device_fn(): pl.pallas_call(restore, out_shape=jax.ShapeDtypeStruct((ROWS, HALF), BF16...  2.61 us

profile of v5, /device:TPU:1, one launch (start us, length us, event | category | flops | bytes accessed | tf_op | source)
XLA Modules:
  0.0 75.1 jit_solution(7786498581289956578)
XLA Ops:
  0.0 72.5 %dilated.1.outp = bf16[1024,512]{1,0:T(8,128)(2,1)} custom-call(bf16[1024,1024]{1,0:T(8,128)(2,1)} %hid.1, bf16[1024,512]{1,0:T(8,128)(2,1)} %wq.1, bf16[1024,512]{1,0:T(8,128)(2,1)} %wk.1, bf16[1024,512]{1,0:T(8,128)(2,1)} %wv.1, bf16[512,1024]{1,0:T(8,128)(2,1)} %wo.1, f32[4,16]{1,0:T(4,128)} %bias.1), custom_call_target="tpu_custom_call" | custom-call | tf_op jit(solution)/shard_map/dilated/pallas_call | solution.py:350
  72.5 2.6 %restore.1 = bf16[1024,512]{1,0:T(8,128)(2,1)} custom-call(bf16[1024,512]{1,0:T(8,128)(2,1)} %dilated.1.outp), custom_call_target="tpu_custom_call" | custom-call | tf_op jit(solution)/shard_map/restore/pallas_call | solution.py:373

commit v6 on v5

--- a/solution.py
+++ b/solution.py
@@ -19,18 +19,18 @@
 HALF = 512
 DIM = 64
 KEYS = 2048
-SLOTS = 2
+SLOTS = 3
 
 UNITS = (
-    (0, 0, 0, TILE),
-    (0, 0, TILE, TILE),
-    (0, 0, 2 * TILE, TILE),
-    (0, 0, 3 * TILE, TILE),
+    (0, 0, 0, HALF),
+    (0, 0, HALF, HALF),
     (2, -1, 0, TILE),
-    (1, 0, 0, TILE),
-    (1, 0, TILE, TILE),
+    (1, 0, 0, HALF),
     (3, -1, 0, LANE),
 )
+WIDTHS = (HALF, HALF, TILE)
+SLOT_OF = (0, 1, 2, 0, 2)
+SWAPPED = (1, 0, 2, 1, 2)
 
 
 def nt_dot(a, b):
@@ -64,26 +64,25 @@
     pl.semaphore_signal(barrier, inc=1, device_id={'tp': 1 - tp}, device_id_type=MESH)
 
     def refs(n, h):
-        if n == 0:
-            return own.at[h, pl.ds(0, HALF)], r1.at[h, pl.ds(0, HALF)], 0
-        if n == 1:
-            return own.at[h, pl.ds(HALF, HALF)], r1.at[h, pl.ds(HALF, HALF)], 0
-        if n == 2:
-            return own.at[h, pl.ds(0, HALF)], r2.at[h, pl.ds(0, HALF)], 1
-        if n == 3:
-            return r1.at[h, pl.ds(0, HALF)], r2.at[h, pl.ds(HALF, HALF)], 1
-        if n < 8:
-            src = (own.at[h, pl.ds(0, TILE)], r1.at[h, pl.ds(0, TILE)], r2.at[h, pl.ds(0, TILE)], r2.at[h, pl.ds(HALF, TILE)])[n - 4]
-            return src, r3.at[h, pl.ds((n - 4) * TILE, TILE)], 2
-        if n < 12:
-            src = (own.at[h, pl.ds(0, LANE)], r1.at[h, pl.ds(0, LANE)], r2.at[h, pl.ds(0, LANE)], r2.at[h, pl.ds(HALF, LANE)])[n - 8]
-        else:
-            src = r3.at[h, pl.ds((n - 12) * TILE, LANE)]
-        return src, r4.at[h, pl.ds((n - 8) * LANE, LANE)], 3
+        low4, low2 = pl.ds(0, 4), pl.ds(0, 2)
+        return (
+            lambda: (own.at[h, low4], r1.at[h, low4], 0),
+            lambda: (own.at[h, pl.ds(4, 4)], r1.at[h, pl.ds(4, 4)], 0),
+            lambda: (own.at[h, low4], r2.at[h, :, 0], 1),
+            lambda: (r1.at[h, low4], r2.at[h, :, 1], 1),
+            lambda: (own.at[h, low2], r3.at[h, :, 0], 2),
+            lambda: (r1.at[h, low2], r3.at[h, :, 1], 2),
+            lambda: (r2.at[h, low2], r3.at[h, :, pl.ds(2, 2)], 2),
+            lambda: (own.at[h, 0], r4.at[h, 0], 3),
+            lambda: (r1.at[h, 0], r4.at[h, 1], 3),
+            lambda: (r2.at[h, 0], r4.at[h, pl.ds(2, 2)], 3),
+            lambda: (r3.at[h, 0, low2], r4.at[h, pl.ds(4, 2)], 3),
+            lambda: (r3.at[h, 0, pl.ds(2, 2)], r4.at[h, pl.ds(6, 2)], 3),
+        )[n]()
 
     def copy(n, h):
         src, dst, level = refs(n, h)
-        sem = min(n, 8)
+        sem = min(n, 7)
         return pltpu.make_async_remote_copy(src, dst, ssem.at[level], rsem.at[h, sem], device_id={'sp': peers[level]}, device_id_type=MESH)
 
     def start(h, *chunks):
@@ -94,34 +93,35 @@
         copy(n, h).wait_recv()
 
     def arrive_all(h):
-        pltpu.make_async_remote_copy(r4.at[h], r4.at[h], ssem.at[3], rsem.at[h, 8], device_id={'sp': peers[3]}, device_id_type=MESH).wait_recv()
+        pltpu.make_async_remote_copy(r4.at[h], r4.at[h], ssem.at[3], rsem.at[h, 7], device_id={'sp': peers[3]}, device_id_type=MESH).wait_recv()
 
     def sent(level):
         pltpu.make_async_remote_copy(own, own, ssem.at[level], rsem.at[0, 0], device_id={'sp': peers[level]}, device_id_type=MESH).wait_send()
 
     def event1(h):
         arrive(h, 0)
-        start(h, 3, 5, 9)
-        if isinstance(h, int):
-            if h + 2 < HEADS:
-                start(h + 2, 2, 4, 8)
-        else:
-            @pl.when(h + 2 < HEADS)
-            def _():
-                start(h + 2, 2, 4, 8)
-
-    def event2(h):
+        start(h, 3, 5, 8)
+        guard(h + 2 < HEADS, lambda: start(h + 2, 2, 4, 7))
+
+    def event3(h):
         arrive(h, 2)
-        start(h, 6, 10)
-
-    def event3(h):
         arrive(h, 3)
-        start(h, 7, 11)
-
-    def event4(h, *parts):
-        for c in parts:
-            arrive(h, 4 + c)
-            start(h, 12 + c)
+        start(h, 6, 9)
+
+    def event4(h):
+        arrive(h, 4)
+        arrive(h, 5)
+        start(h, 10)
+
+    def event5(h):
+        arrive(h, 6)
+        start(h, 11)
+
+    def guard(condition, action):
+        if not isinstance(condition, bool):
+            pl.when(condition)(action)
+        elif condition:
+            action()
 
     row_id = lax.broadcasted_iota(jnp.int32, (LANE, LANE), 0)
     col_id = lax.broadcasted_iota(jnp.int32, (LANE, LANE), 1)
@@ -138,7 +138,7 @@
     def place(dst, h, half, value):
         for j in range(4):
             pos = ORDER.index((half * 4 + j - h) % 8)
-            dst[h, pos * LANE:(pos + 1) * LANE, :] = value[j * LANE:(j + 1) * LANE, :]
+            dst[h, pos] = value[j * LANE:(j + 1) * LANE, :]
 
     def project_kv(cols):
         for half in range(2):
@@ -166,7 +166,7 @@
     project_kv(0)
     pl.semaphore_wait(barrier, 5)
     for h in range(2):
-        start(h, 0, 1, 2, 4, 8)
+        start(h, 0, 1, 2, 4, 7)
     for h in range(2, 4):
         start(h, 0, 1)
     project_kv(1)
@@ -183,20 +183,18 @@
     o_t[...] = jnp.zeros_like(o_t)
 
     def keys(branch, h):
-        if branch == 0:
-            parts = [own[h], r1[h]]
-        elif branch == 1:
-            parts = [own[h, 0:HALF, :], r1[h, 0:HALF, :], r2[h]]
-        elif branch == 2:
-            parts = [own[h, 0:TILE, :], r1[h, 0:TILE, :], r2[h, 0:TILE, :], r2[h, HALF:768, :], r3[h]]
-        else:
-            parts = [own[h, 0:LANE, :], r1[h, 0:LANE, :], r2[h, 0:LANE, :], r2[h, HALF:640, :]]
-            parts += [r3[h, c * TILE:c * TILE + LANE, :] for c in range(4)] + [r4[h]]
-        return jnp.concatenate(parts, axis=0)
+        count = 8 >> branch
+        parts = [own[h, 0:count], r1[h, 0:count]]
+        for level, held in ((1, r2), (2, r3), (3, r4)):
+            if branch > level:
+                parts.append(held[h, 0:count])
+            elif branch == level:
+                parts.append(held[h])
+        return jnp.concatenate([p.reshape(p.size // LANE, LANE) for p in parts], axis=0)
 
     def logits(unit, slot):
         branch, h, first, rows = unit
-        s = nt_dot(keys(branch, h), q_s[h, first:first + rows, :])
+        s = nt_dot(keys(branch, h), q_s[h, first // LANE:(first + rows) // LANE].reshape(rows, LANE))
         S[slot][:, 0:rows] = s
         M[slot][:, 0:rows] = jnp.broadcast_to(jnp.max(s, axis=0, keepdims=True), (SUB, rows))
 
@@ -250,8 +248,7 @@
         branch, shift, first, rows = UNITS[u]
         return branch, h + shift, first, rows
 
-    def push(flight, unit):
-        slot = (flight[-1][1] + 1) % SLOTS if flight else 0
+    def push(flight, unit, slot):
         pl.delay(1)
         logits(unit, slot)
         if flight:
@@ -259,58 +256,47 @@
             gain(*flight[-1])
         return [(unit, slot)], flight[-1][0] if flight else None
 
-    def run(flight, h, *which):
+    def run(flight, h, *which, slots=SLOT_OF):
         for u in which:
-            flight, done = push(flight, unit_of(u, h))
+            flight, done = push(flight, unit_of(u, h), slots[u])
             if done is not None and done[0] == 3:
                 finish(done[1])
         return flight
 
     event1(0)
-    event2(0)
     arrive(0, 1)
-    flight = run([], 0, 0)
-    event2(1)
-    flight = run(flight, 0, 1, 2, 3)
+    flight = run([], 0, 0, 1, slots=SWAPPED)
     event3(0)
     event1(1)
-    event4(0, 0, 1, 2)
-    flight = run(flight, 0, 5, 6)
-
-    def guard(condition, action):
-        if not isinstance(condition, bool):
-            pl.when(condition)(action)
-        elif condition:
-            action()
+    event4(0)
+    flight = run(flight, 0, 3, slots=SWAPPED)
 
     def pass_of(h, flight):
         arrive(h, 1)
         flight = run(flight, h, 0)
-        guard(h + 1 < HEADS, lambda: event2(h + 1))
         guard((h >= 3) & (h % 2 == 1), lambda: send_o((h - 3) // 2).start())
-        flight = run(flight, h, 1)
-        event4(h - 1, 3)
-        flight = run(flight, h, 2, 3, 4)
+        event5(h - 1)
+        flight = run(flight, h, 1, 2)
         event3(h)
         guard(h + 1 < HEADS, lambda: event1(h + 1))
-        event4(h, 0, 1, 2)
-        flight = run(flight, h, 5, 6)
+        event4(h)
+        flight = run(flight, h, 3)
         arrive_all(h - 1)
-        return run(flight, h, 7)
+        return run(flight, h, 4)
 
     flight = pass_of(1, flight)
 
     def body(h, carry):
-        left = pass_of(h, [(unit_of(7, h - 1), flight[0][1])])
+        left = pass_of(h, [(unit_of(4, h - 1), flight[0][1])])
         assert left[0][1] == flight[0][1]
         return carry
 
     lax.fori_loop(2, HEADS, body, 0)
-    flight = [(unit_of(7, HEADS - 1), flight[0][1])]
-    event4(HEADS - 1, 3)
+    flight = [(unit_of(4, HEADS - 1), flight[0][1])]
+    event5(HEADS - 1)
+    flight = run(flight, HEADS, 2, slots=(0,) * 3)
+    arrive_all(HEADS - 1)
     flight = run(flight, HEADS, 4)
-    arrive_all(HEADS - 1)
-    flight = run(flight, HEADS, 7)
     soften(*flight[0])
     gain(*flight[0])
     finish(HEADS - 1)
@@ -346,7 +332,7 @@
 
 def solution(mesh):
     def device_fn(hidden, w_query, w_key, w_value, w_out, branch_bias):
-        kv = pltpu.VMEM((HEADS, ROWS, LANE), BF16)
+        kv, kv2, kv3 = (pltpu.VMEM((HEADS, *lead, LANE, LANE), BF16) for lead in ((8,), (4, 2), (2, 4)))
         permuted = pl.pallas_call(
             kernel,
             out_shape=jax.ShapeDtypeStruct((ROWS, HALF), BF16),
@@ -357,14 +343,14 @@
                 pltpu.VMEM((1024, HALF), BF16), pltpu.VMEM((1024, HALF), BF16), pltpu.VMEM((1024, HALF), BF16),
                 pltpu.VMEM((HALF, 1024), BF16), pltpu.VMEM((HALF, HALF), BF16),
                 pltpu.VMEM((ROWS, 1024), BF16),
-                kv, kv, kv, kv, kv, kv,
-                *[pltpu.VMEM((KEYS, TILE), F32)] * SLOTS, *[pltpu.VMEM((KEYS, TILE), BF16)] * SLOTS,
-                *[pltpu.VMEM((SUB, TILE), F32)] * (3 * SLOTS),
+                kv, kv, kv, kv2, kv3, kv,
+                *[pltpu.VMEM((KEYS, n), F32) for n in WIDTHS], *[pltpu.VMEM((KEYS, n), BF16) for n in WIDTHS],
+                *[pltpu.VMEM((SUB, n), F32) for n in WIDTHS * 3],
                 pltpu.VMEM((4, LANE, ROWS), F32), pltpu.VMEM((4, SUB, ROWS), F32), pltpu.VMEM((4, SUB, ROWS), F32), pltpu.VMEM((4, LANE, ROWS), F32),
                 pltpu.VMEM((4, ROWS, LANE), BF16), pltpu.VMEM((4, ROWS, LANE), BF16),
                 pltpu.VMEM((ROWS, HALF), F32),
                 pltpu.SemaphoreType.DMA((5,)),
-                pltpu.SemaphoreType.DMA((4,)), pltpu.SemaphoreType.DMA((HEADS, 9)),
+                pltpu.SemaphoreType.DMA((4,)), pltpu.SemaphoreType.DMA((HEADS, 8)),
                 pltpu.SemaphoreType.DMA((5,)), pltpu.SemaphoreType.DMA((5,)),
             ],
             compiler_params=pltpu.CompilerParams(collective_id=0, has_side_effects=True, vmem_limit_bytes=62 * 1024 * 1024),

time: 75.3 us -> 80 us (1.062)
  Pallas kernels: 75.1 us -> 79.8 us
    pallas_call x1, Pallas kernels: 72.5 us -> 77.2 us  [device_fn(): pl.pallas_call(kernel, out_shape=jax.ShapeDtypeStruct((ROWS, HALF), BF16)...]
where the time goes in v6:
time: 80 us; the launch traced here: 79.9 us
  Pallas kernels  79.8 us (100%)
    pallas_call x1, Pallas kernels, device_fn(): pl.pallas_call(kernel, out_shape=jax.ShapeDtypeStruct((ROWS, HALF), BF16)...  77.2 us
    pallas_call x1, Pallas kernels, device_fn(): pl.pallas_call(restore, out_shape=jax.ShapeDtypeStruct((ROWS, HALF), BF16...  2.62 us

profile of v6, /device:TPU:1, one launch (start us, length us, event | category | flops | bytes accessed | tf_op | source)
XLA Modules:
  0.0 79.9 jit_solution(15633822022140481636)
XLA Ops:
  0.0 77.2 %dilated.1.outp = bf16[1024,512]{1,0:T(8,128)(2,1)} custom-call(bf16[1024,1024]{1,0:T(8,128)(2,1)} %hid.1, bf16[1024,512]{1,0:T(8,128)(2,1)} %wq.1, bf16[1024,512]{1,0:T(8,128)(2,1)} %wk.1, bf16[1024,512]{1,0:T(8,128)(2,1)} %wv.1, bf16[512,1024]{1,0:T(8,128)(2,1)} %wo.1, f32[4,16]{1,0:T(4,128)} %bias.1), custom_call_target="tpu_custom_call" | custom-call | tf_op jit(solution)/shard_map/dilated/pallas_call | solution.py:336
  77.2 2.6 %restore.1 = bf16[1024,512]{1,0:T(8,128)(2,1)} custom-call(bf16[1024,512]{1,0:T(8,128)(2,1)} %dilated.1.outp), custom_call_target="tpu_custom_call" | custom-call | tf_op jit(solution)/shard_map/restore/pallas_call | solution.py:359

commit v7 on v5

--- a/solution.py
+++ b/solution.py
@@ -55,7 +55,7 @@
     peers = (sp + 1 - 2 * (x % 2), sp + 3 - 2 * x, sp + 4 * (1 - 2 * (y % 2)), sp + 4 * (3 - 2 * y))
 
     loads = [pltpu.make_async_copy(a, b, in_sem.at[n]) for n, (a, b) in enumerate(((hid, hid_v), (wk, wk_v), (wv, wv_v), (wq, wq_v), (wo, wo_v)))]
-    for load in loads:
+    for load in loads[:3]:
         load.start()
 
     barrier = pltpu.get_barrier_semaphore()
@@ -128,6 +128,8 @@
     gather = jnp.where(col_id == 8 * (row_id % 16) + row_id // 16, 1.0, 0.0).astype(BF16)
 
     loads[0].wait()
+    for load in loads[3:]:
+        load.start()
     for c in range(8):
         part = nn_dot(gather, hid_v[c * LANE:(c + 1) * LANE, :]).astype(BF16)
         for r in range(8):
@@ -139,6 +141,18 @@
         for j in range(4):
             pos = ORDER.index((half * 4 + j - h) % 8)
             dst[h, pos * LANE:(pos + 1) * LANE, :] = value[j * LANE:(j + 1) * LANE, :]
+
+    def place_kv(h, half, kp, vp):
+        vp = pltpu.roll(vp, DIM, 1)
+        place(own, h, half, jnp.where(low, kp, vp).astype(BF16))
+        place(own, h + 1, half, jnp.where(low, vp, kp).astype(BF16))
+
+    def project_pair(a):
+        at = slice(a * LANE, (a + 1) * LANE)
+        both = jnp.concatenate([wk_v[:, at], wv_v[:, at]], axis=1)
+        for half in range(2):
+            got = nn_dot(xp[half * HALF:(half + 1) * HALF, :], both)
+            place_kv(2 * a, half, got[:, 0:LANE], got[:, LANE:TILE])
 
     def project_kv(cols):
         for half in range(2):
@@ -146,11 +160,8 @@
             key = nn_dot(rows, wk_v[:, cols * TILE:(cols + 1) * TILE])
             val = nn_dot(rows, wv_v[:, cols * TILE:(cols + 1) * TILE])
             for a in range(2):
-                h = 4 * cols + 2 * a
-                kp = key[:, a * LANE:(a + 1) * LANE]
-                vp = pltpu.roll(val[:, a * LANE:(a + 1) * LANE], DIM, 1)
-                place(own, h, half, jnp.where(low, kp, vp).astype(BF16))
-                place(own, h + 1, half, jnp.where(low, vp, kp).astype(BF16))
+                at = slice(a * LANE, (a + 1) * LANE)
+                place_kv(4 * cols + 2 * a, half, key[:, at], val[:, at])
 
     def project_q(cols):
         for half in range(2):
@@ -163,10 +174,11 @@
 
     loads[1].wait()
     loads[2].wait()
-    project_kv(0)
+    project_pair(0)
     pl.semaphore_wait(barrier, 5)
     for h in range(2):
         start(h, 0, 1, 2, 4, 8)
+    project_pair(1)
     for h in range(2, 4):
         start(h, 0, 1)
     project_kv(1)

time: 75.3 us -> 74.6 us (level)
  no operation moved by 1% of the time
where the time goes in v7:
time: 74.6 us; the launch traced here: 74.5 us
  Pallas kernels  74.5 us (100%)
    pallas_call x1, Pallas kernels, device_fn(): pl.pallas_call(kernel, out_shape=jax.ShapeDtypeStruct((ROWS, HALF), BF16)...  71.9 us
    pallas_call x1, Pallas kernels, device_fn(): pl.pallas_call(restore, out_shape=jax.ShapeDtypeStruct((ROWS, HALF), BF16...  2.62 us

profile of v7, /device:TPU:1, one launch (start us, length us, event | category | flops | bytes accessed | tf_op | source)
XLA Modules:
  0.0 74.5 jit_solution(17046447682624797477)
XLA Ops:
  0.0 71.9 %dilated.1.outp = bf16[1024,512]{1,0:T(8,128)(2,1)} custom-call(bf16[1024,1024]{1,0:T(8,128)(2,1)} %hid.1, bf16[1024,512]{1,0:T(8,128)(2,1)} %wq.1, bf16[1024,512]{1,0:T(8,128)(2,1)} %wk.1, bf16[1024,512]{1,0:T(8,128)(2,1)} %wv.1, bf16[512,1024]{1,0:T(8,128)(2,1)} %wo.1, f32[4,16]{1,0:T(4,128)} %bias.1), custom_call_target="tpu_custom_call" | custom-call | tf_op jit(solution)/shard_map/dilated/pallas_call | solution.py:362
  71.9 2.6 %restore.1 = bf16[1024,512]{1,0:T(8,128)(2,1)} custom-call(bf16[1024,512]{1,0:T(8,128)(2,1)} %dilated.1.outp), custom_call_target="tpu_custom_call" | custom-call | tf_op jit(solution)/shard_map/restore/pallas_call | solution.py:385
